TPU v7x, 512 devices: a whole 4x8x8 slice. The times are simulated.
512 devices in a mesh: batch: 128 (over x, y_lo, z), mp: 4 (over y_hi, core).
Axes of the slice: x: 4, y: 8 (y_hi: 2, y_lo: 4; y = y_hi * 4 + y_lo), z: 8, core: 2. Of those that a mesh axis runs over, the one named last changes fastest.
Arguments:
- img_feat: bfloat16 [2048, 1536], P('batch'), may hold values from -6 to 6
- txt_feat: bfloat16 [2048, 1536], P('batch'), may hold values from -6 to 6
- w_img: bfloat16 [1536, 1152], P('batch', 'mp'), may hold values from -0.15625 to 0.15625
- w_txt: bfloat16 [1536, 1152], P('batch', 'mp'), may hold values from -0.15625 to 0.15625
- pair_index: int32 [2048], P('batch'), may hold values from 0 to 2047, each once
- log_scale: float32 [1], replicated, may hold values from 2 to 2.6
- bias: float32 [1], replicated, may hold values from -6 to -4
Outputs:
- image_grad: float32 [2048, 1152], P('batch', 'mp')
- text_grad: float32 [2048, 1152], P(('batch', 'mp'))
Inputs may be any that keep to these rules, and one draw needn't show every extreme that they name: `pair_index`: each text index appears exactly once.
All inputs are finite; a program needn't handle non-finite values.
Results may differ from a plain program's by a relative error of at most 0.0046.
Values may be sent and summed in bfloat16 or wider, within the bound.
No kernel may reach another device: no remote copies, remote signals or barrier semaphores. Data moves between devices by JAX's collectives and lax.ppermute only.
A program may use at most 64 MiB of HBM per device.

v0:
```python
import jax
import jax.numpy as jnp
from jax import lax
from jax.sharding import Mesh
from jax.sharding import PartitionSpec as P

BATCH = ("batch_0", "batch_1", "batch_2")
MP = ("mp_0", "mp_1")
BATCH_MP = ("batch_0", "batch_1", "batch_2", "mp_0", "mp_1")
epsilon = 1e-06


def joined_along(pieces, dim):
    lengths = list(pieces.shape[1:])
    lengths[dim] *= pieces.shape[0]
    return jnp.moveaxis(pieces, 0, dim).reshape(lengths)


def stacked_from(x, axes, order):
    pieces = x[None]
    for k in order:
        pieces = lax.all_gather(pieces, axes[k], axis=0, tiled=True)
    current = [lax.axis_size(axes[k]) for k in reversed(order)]
    pieces = pieces.reshape(*current, *x.shape)
    turned = sorted(range(len(order)), key=lambda place: order[len(order) - 1 - place])
    return pieces.transpose(*turned, *range(len(order), pieces.ndim)).reshape(-1, *x.shape)


def gathered_by_axis(x, axes, order, dim):
    return joined_along(stacked_from(x, axes, order), dim)


def from_behind(value, axis, steps):
    count = lax.axis_size(axis)
    pairs = [(source, (source + steps) % count) for source in range(count)]
    return lax.ppermute(value, axis, pairs)


def in_blocks(x, dim, size):
    before, after = (x.shape[:dim], x.shape[dim + 1 :])
    return jnp.moveaxis(x.reshape(*before, size, -1, *after), dim, 0)


def sent_and_summed(x, axis, dim):
    pieces = in_blocks(x, dim, lax.axis_size(axis))
    arrived = lax.all_to_all(pieces, axis, split_axis=0, concat_axis=0, tiled=True)
    return arrived.sum(axis=0)


def normalize(pre):
    values = pre.astype(jnp.float32)
    norm = lax.rsqrt(jnp.sum(values * values, axis=1, keepdims=True) + epsilon)
    return (values * norm).astype(jnp.bfloat16)


def block_update(image, pairing, scale, offset, text, first):
    count = text.shape[0]
    scores = lax.dot_general(
        image, text, (((1,), (1,)), ((), ())), preferred_element_type=jnp.float32
    )
    logits = scale * scores + offset
    columns = first + jnp.arange(count, dtype=jnp.int32)
    label = jnp.where(pairing[:, None] == columns[None, :], 1.0, -1.0).astype(jnp.float32)
    coef = (-label * jax.nn.sigmoid(-label * logits)).astype(jnp.bfloat16)
    image_term = jnp.dot(coef, text, preferred_element_type=jnp.float32)
    text_term = lax.dot_general(
        coef, image, (((0,), (0,)), ((), ())), preferred_element_type=jnp.float32
    )
    return (image_term, text_term)


def local(img_feat, txt_feat, w_img, w_txt, pair_index, log_scale, bias):
    rows = img_feat.shape[0]
    cycle_size = lax.axis_size(BATCH)
    group_size = lax.axis_size(MP)
    here = lax.axis_index(BATCH)
    member = lax.axis_index(MP)
    piece_rows = rows // group_size
    columns_part = w_img.shape[1]
    width = group_size * columns_part
    span = min(cycle_size, 32)
    half = span // 2
    first = jnp.dot(
        img_feat, gathered_by_axis(w_img, BATCH, (1, 2, 0), 0), preferred_element_type=jnp.float32
    )
    second = jnp.dot(
        txt_feat, gathered_by_axis(w_txt, BATCH, (1, 2, 0), 0), preferred_element_type=jnp.float32
    )
    full_img, full_txt = (
        gathered_by_axis(first.astype(jnp.bfloat16), MP, (0, 1), 1),
        gathered_by_axis(second.astype(jnp.bfloat16), MP, (0, 1), 1),
    )
    image = normalize(full_img)
    own_start = member * piece_rows
    text = normalize(lax.dynamic_slice_in_dim(full_txt, own_start, piece_rows, 0))
    scale = jnp.exp(log_scale[0])
    offset = bias[0]
    image_total = jnp.zeros((rows, width), jnp.float32)
    start_grads = jnp.zeros((piece_rows, width), jnp.float32)

    def first_row(anchor):
        return anchor * rows + member * piece_rows

    def turn_front(step, carry):
        front, front_acc, totals = carry
        anchor = (here - step) % cycle_size
        image_term, text_term = block_update(
            image, pair_index, scale, offset, front, first_row(anchor)
        )
        front = from_behind(front, BATCH, 1)
        front_acc = from_behind(front_acc + text_term, BATCH, 1)
        return (front, front_acc, totals + image_term)

    def turn_rear(step, carry):
        rear, rear_acc, totals = carry
        rear = from_behind(rear, BATCH, -1)
        rear_acc = from_behind(rear_acc, BATCH, -1)
        anchor = (here + step + 1) % cycle_size
        image_term, text_term = block_update(
            image, pair_index, scale, offset, rear, first_row(anchor)
        )
        return (rear, rear_acc + text_term, totals + image_term)

    front, front_acc, image_total = lax.fori_loop(
        0, half, turn_front, (text, start_grads, image_total)
    )
    rear, rear_acc, image_total = lax.fori_loop(
        0, half, turn_rear, (text, start_grads, image_total)
    )
    front_back = from_behind(front_acc, BATCH, -half)
    rear_back = from_behind(rear_acc, BATCH, half)
    text_total = front_back + rear_back
    image_part = sent_and_summed(image_total, MP, 1)
    return (scale * image_part, scale * text_total)


def solution(mesh):
    finer = Mesh(
        mesh.devices.reshape(4, 4, 8, 2, 2), ("batch_0", "batch_1", "batch_2", "mp_0", "mp_1")
    )
    in_specs = (P(BATCH, None), P(BATCH, None), P(BATCH, MP), P(BATCH, MP), P(BATCH), P(), P())
    out_specs = (P(BATCH, MP), P(BATCH_MP, None))
    return jax.shard_map(local, mesh=finer, in_specs=in_specs, out_specs=out_specs, check_vma=False)
```

profile of v0, /device:TPU:1, one launch (start us, length us, event | category | flops | bytes accessed | tf_op | source)
XLA Modules:
  0.0 614.7 jit_solution(6283159459050296204)
XLA Ops:
  0.7 11.5 %all-gather.4 = bf16[4,12,288]{2,1,0:T(8,128)(2,1)S(1)} all-gather(bf16[1,12,288]{2,1,0:T(8,128)(2,1)} %bitcast.76), channel_id=2, replica_groups=mesh['batch_0'=4,'batch_1'=4,'batch_2'=8,'mp_0'=2,'mp_1'=2] {'batch_1'}, dimensions={0}, use_global_device_ids=true | all-gather | bytes 34560 | tf_op jit(solution)/shard_map/all_gather | solution.py:22
  12.1 26.0 %all_gather.31 = bf16[32,12,288]{2,1,0:T(8,128)(2,1)S(1)} all-gather(bf16[4,12,288]{2,1,0:T(8,128)(2,1)S(1)} %all-gather.4), channel_id=1, replica_groups=mesh['batch_0'=4,'batch_1'=4,'batch_2'=8,'mp_0'=2,'mp_1'=2] {'batch_2'}, dimensions={0}, use_global_device_ids=true | all-gather | bytes 248832 | tf_op jit(solution)/shard_map/all_gather | solution.py:22
  38.2 12.2 %all_gather.32 = bf16[128,12,288]{2,0,1:T(8,128)(2,1)S(1)} all-gather(bf16[32,12,288]{2,0,1:T(8,128)(2,1)S(1)} %copy.24), channel_id=1, replica_groups=mesh['batch_0'=4,'batch_1'=4,'batch_2'=8,'mp_0'=2,'mp_1'=2] {'batch_0'}, dimensions={0}, use_global_device_ids=true | all-gather | bytes 1105920 | tf_op jit(solution)/shard_map/all_gather | solution.py:22
  52.4 7.2 %all-gather.1 = bf16[32,288]{1,0:T(8,128)(2,1)S(1)} all-gather(bf16[16,288]{1,0:T(8,128)(2,1)S(1)} %convolution_convert_fusion.1), channel_id=3, replica_groups=mesh['batch_0'=4,'batch_1'=4,'batch_2'=8,'mp_0'=2,'mp_1'=2] {'mp_0'}, dimensions={0}, use_global_device_ids=true | all-gather | bytes 27648 | tf_op jit(solution)/shard_map/all_gather | solution.py:22
  59.6 14.0 %all_gather.34 = bf16[4,16,288]{2,1,0:T(8,128)(2,1)S(1)} all-gather(bf16[2,16,288]{2,1,0:T(8,128)(2,1)S(1)} %bitcast.74), channel_id=1, replica_groups=mesh['batch_0'=4,'batch_1'=4,'batch_2'=8,'mp_0'=2,'mp_1'=2] {'mp_1'}, dimensions={0}, use_global_device_ids=true | all-gather | bytes 55296 | tf_op jit(solution)/shard_map/all_gather | solution.py:22
  73.9 10.2 %all-gather.5 = bf16[4,12,288]{2,1,0:T(8,128)(2,1)S(1)} all-gather(bf16[1,12,288]{2,1,0:T(8,128)(2,1)S(1)} %bitcast.77), channel_id=4, replica_groups=mesh['batch_0'=4,'batch_1'=4,'batch_2'=8,'mp_0'=2,'mp_1'=2] {'batch_1'}, dimensions={0}, use_global_device_ids=true | all-gather | bytes 34560 | tf_op jit(solution)/shard_map/all_gather | solution.py:22
  84.2 19.4 %all_gather.36 = bf16[32,12,288]{2,1,0:T(8,128)(2,1)S(1)} all-gather(bf16[4,12,288]{2,1,0:T(8,128)(2,1)S(1)} %all-gather.5), channel_id=1, replica_groups=mesh['batch_0'=4,'batch_1'=4,'batch_2'=8,'mp_0'=2,'mp_1'=2] {'batch_2'}, dimensions={0}, use_global_device_ids=true | all-gather | bytes 248832 | tf_op jit(solution)/shard_map/all_gather | solution.py:22
  103.6 11.8 %all_gather.37 = bf16[128,12,288]{2,0,1:T(8,128)(2,1)S(1)} all-gather(bf16[32,12,288]{2,0,1:T(8,128)(2,1)S(1)} %copy.28), channel_id=1, replica_groups=mesh['batch_0'=4,'batch_1'=4,'batch_2'=8,'mp_0'=2,'mp_1'=2] {'batch_0'}, dimensions={0}, use_global_device_ids=true | all-gather | bytes 1105920 | tf_op jit(solution)/shard_map/all_gather | solution.py:22
  117.5 7.2 %all-gather.3 = bf16[32,288]{1,0:T(8,128)(2,1)S(1)} all-gather(bf16[16,288]{1,0:T(8,128)(2,1)S(1)} %convolution_convert_fusion), channel_id=5, replica_groups=mesh['batch_0'=4,'batch_1'=4,'batch_2'=8,'mp_0'=2,'mp_1'=2] {'mp_0'}, dimensions={0}, use_global_device_ids=true | all-gather | bytes 27648 | tf_op jit(solution)/shard_map/all_gather | solution.py:22
  124.7 14.2 %all_gather.39 = bf16[4,16,288]{2,1,0:T(8,128)(2,1)S(1)} all-gather(bf16[2,16,288]{2,1,0:T(8,128)(2,1)S(1)} %bitcast.75), channel_id=1, replica_groups=mesh['batch_0'=4,'batch_1'=4,'batch_2'=8,'mp_0'=2,'mp_1'=2] {'mp_1'}, dimensions={0}, use_global_device_ids=true | all-gather | bytes 55296 | tf_op jit(solution)/shard_map/all_gather | solution.py:22
  140.0 215.3 %while.40 = (s32[]{:T(128)}, bf16[4,1152]{1,0:T(4,128)(2,1)S(1)}, f32[4,1152]{1,0:T(4,128)S(1)}, f32[16,1152]{1,0:T(8,128)S(1)}, s32[16]{0:T(128)S(1)}, /*index=...) while((s32[]{:T(128)}, bf16[4,1152]{1,0:T(4,128)(2,1)S(1)}, ...), condition=%wide.region_3.4_spmd.clone, body=%wide.region_2.3_spmd.clone.sunk | while | flops 484565 | bytes 406372 | solution.py:124
  140.0 2.9 collective-permute-start
  146.0 4.4 collective-permute-done
  150.4 3.9 collective-permute-done.1
  159.4 5.4 collective-permute-done
  164.8 3.0 collective-permute-done.1
  172.8 5.4 collective-permute-done
  178.2 3.0 collective-permute-done.1
  186.2 5.4 collective-permute-done
  191.6 3.0 collective-permute-done.1
  199.6 5.4 collective-permute-done
  205.0 3.0 collective-permute-done.1
  213.0 5.4 collective-permute-done
  218.4 3.0 collective-permute-done.1
  226.4 5.4 collective-permute-done
  231.8 3.0 collective-permute-done.1
  239.7 5.4 collective-permute-done
  245.2 3.0 collective-permute-done.1
  253.1 5.4 collective-permute-done
  258.5 3.0 collective-permute-done.1
  266.5 5.6 collective-permute-done
  272.1 2.8 collective-permute-done.1
  279.9 5.4 collective-permute-done
  285.3 3.0 collective-permute-done.1
  293.3 5.4 collective-permute-done
  298.7 3.0 collective-permute-done.1
  306.7 5.4 collective-permute-done
  312.1 3.0 collective-permute-done.1
  320.1 5.4 collective-permute-done
  325.5 3.0 collective-permute-done.1
  333.5 5.4 collective-permute-done
  338.9 3.0 collective-permute-done.1
  346.9 5.4 collective-permute-done
  352.3 3.0 collective-permute-done.1
  355.3 196.7 %while.41 = (s32[]{:T(128)}, bf16[4,1152]{1,0:T(4,128)(2,1)S(1)}, f32[4,1152]{1,0:T(4,128)S(1)}, f32[16,1152]{1,0:T(8,128)S(1)}, s32[16]{0:T(128)S(1)}, /*index=...) while((s32[]{:T(128)}, bf16[4,1152]{1,0:T(4,128)(2,1)S(1)}, ...), condition=%wide.region_5.6_spmd.clone, body=%wide.region_4.5_spmd.clone.sunk | while | flops 470742 | bytes 443248 | solution.py:127
  355.3 3.4 collective-permute-start.2
  363.3 7.9 %collective-permute-start.2 = (bf16[4,1152]{1,0:T(4,128)(2,1)S(1)}, bf16[4,1152]{1,0:T(4,128)(2,1)S(1)}, u32[]{:S(2)}, u32[]{:S(2)}) collective-permute-start(bf16[4,1152]{1,0:T(4,128)(2,1)S(1)} %get-tuple-element.787), channel_id=1, source_target_pairs={{0,508},{4,0},{8,4},{12,8},{16,12},{20,16},{24,20},{28,24},{32,28}... | collective-permute-start | bytes 27656 | tf_op jit(solution)/shard_map/while/body/eval_jaxpr/ppermute | solution.py:36
  375.8 7.9 %collective-permute-start.2 = (bf16[4,1152]{1,0:T(4,128)(2,1)S(1)}, bf16[4,1152]{1,0:T(4,128)(2,1)S(1)}, u32[]{:S(2)}, u32[]{:S(2)}) collective-permute-start(bf16[4,1152]{1,0:T(4,128)(2,1)S(1)} %get-tuple-element.787), channel_id=1, source_target_pairs={{0,508},{4,0},{8,4},{12,8},{16,12},{20,16},{24,20},{28,24},{32,28}... | collective-permute-start | bytes 27656 | tf_op jit(solution)/shard_map/while/body/eval_jaxpr/ppermute | solution.py:36
  388.4 7.9 %collective-permute-start.2 = (bf16[4,1152]{1,0:T(4,128)(2,1)S(1)}, bf16[4,1152]{1,0:T(4,128)(2,1)S(1)}, u32[]{:S(2)}, u32[]{:S(2)}) collective-permute-start(bf16[4,1152]{1,0:T(4,128)(2,1)S(1)} %get-tuple-element.787), channel_id=1, source_target_pairs={{0,508},{4,0},{8,4},{12,8},{16,12},{20,16},{24,20},{28,24},{32,28}... | collective-permute-start | bytes 27656 | tf_op jit(solution)/shard_map/while/body/eval_jaxpr/ppermute | solution.py:36
  401.0 7.9 %collective-permute-start.2 = (bf16[4,1152]{1,0:T(4,128)(2,1)S(1)}, bf16[4,1152]{1,0:T(4,128)(2,1)S(1)}, u32[]{:S(2)}, u32[]{:S(2)}) collective-permute-start(bf16[4,1152]{1,0:T(4,128)(2,1)S(1)} %get-tuple-element.787), channel_id=1, source_target_pairs={{0,508},{4,0},{8,4},{12,8},{16,12},{20,16},{24,20},{28,24},{32,28}... | collective-permute-start | bytes 27656 | tf_op jit(solution)/shard_map/while/body/eval_jaxpr/ppermute | solution.py:36
  413.6 7.9 %collective-permute-start.2 = (bf16[4,1152]{1,0:T(4,128)(2,1)S(1)}, bf16[4,1152]{1,0:T(4,128)(2,1)S(1)}, u32[]{:S(2)}, u32[]{:S(2)}) collective-permute-start(bf16[4,1152]{1,0:T(4,128)(2,1)S(1)} %get-tuple-element.787), channel_id=1, source_target_pairs={{0,508},{4,0},{8,4},{12,8},{16,12},{20,16},{24,20},{28,24},{32,28}... | collective-permute-start | bytes 27656 | tf_op jit(solution)/shard_map/while/body/eval_jaxpr/ppermute | solution.py:36
  426.2 7.9 %collective-permute-start.2 = (bf16[4,1152]{1,0:T(4,128)(2,1)S(1)}, bf16[4,1152]{1,0:T(4,128)(2,1)S(1)}, u32[]{:S(2)}, u32[]{:S(2)}) collective-permute-start(bf16[4,1152]{1,0:T(4,128)(2,1)S(1)} %get-tuple-element.787), channel_id=1, source_target_pairs={{0,508},{4,0},{8,4},{12,8},{16,12},{20,16},{24,20},{28,24},{32,28}... | collective-permute-start | bytes 27656 | tf_op jit(solution)/shard_map/while/body/eval_jaxpr/ppermute | solution.py:36
  438.8 7.9 %collective-permute-start.2 = (bf16[4,1152]{1,0:T(4,128)(2,1)S(1)}, bf16[4,1152]{1,0:T(4,128)(2,1)S(1)}, u32[]{:S(2)}, u32[]{:S(2)}) collective-permute-start(bf16[4,1152]{1,0:T(4,128)(2,1)S(1)} %get-tuple-element.787), channel_id=1, source_target_pairs={{0,508},{4,0},{8,4},{12,8},{16,12},{20,16},{24,20},{28,24},{32,28}... | collective-permute-start | bytes 27656 | tf_op jit(solution)/shard_map/while/body/eval_jaxpr/ppermute | solution.py:36
  451.3 7.9 %collective-permute-start.2 = (bf16[4,1152]{1,0:T(4,128)(2,1)S(1)}, bf16[4,1152]{1,0:T(4,128)(2,1)S(1)}, u32[]{:S(2)}, u32[]{:S(2)}) collective-permute-start(bf16[4,1152]{1,0:T(4,128)(2,1)S(1)} %get-tuple-element.787), channel_id=1, source_target_pairs={{0,508},{4,0},{8,4},{12,8},{16,12},{20,16},{24,20},{28,24},{32,28}... | collective-permute-start | bytes 27656 | tf_op jit(solution)/shard_map/while/body/eval_jaxpr/ppermute | solution.py:36
  463.9 7.9 %collective-permute-start.2 = (bf16[4,1152]{1,0:T(4,128)(2,1)S(1)}, bf16[4,1152]{1,0:T(4,128)(2,1)S(1)}, u32[]{:S(2)}, u32[]{:S(2)}) collective-permute-start(bf16[4,1152]{1,0:T(4,128)(2,1)S(1)} %get-tuple-element.787), channel_id=1, source_target_pairs={{0,508},{4,0},{8,4},{12,8},{16,12},{20,16},{24,20},{28,24},{32,28}... | collective-permute-start | bytes 27656 | tf_op jit(solution)/shard_map/while/body/eval_jaxpr/ppermute | solution.py:36
  476.5 7.9 %collective-permute-start.2 = (bf16[4,1152]{1,0:T(4,128)(2,1)S(1)}, bf16[4,1152]{1,0:T(4,128)(2,1)S(1)}, u32[]{:S(2)}, u32[]{:S(2)}) collective-permute-start(bf16[4,1152]{1,0:T(4,128)(2,1)S(1)} %get-tuple-element.787), channel_id=1, source_target_pairs={{0,508},{4,0},{8,4},{12,8},{16,12},{20,16},{24,20},{28,24},{32,28}... | collective-permute-start | bytes 27656 | tf_op jit(solution)/shard_map/while/body/eval_jaxpr/ppermute | solution.py:36
  489.1 7.9 %collective-permute-start.2 = (bf16[4,1152]{1,0:T(4,128)(2,1)S(1)}, bf16[4,1152]{1,0:T(4,128)(2,1)S(1)}, u32[]{:S(2)}, u32[]{:S(2)}) collective-permute-start(bf16[4,1152]{1,0:T(4,128)(2,1)S(1)} %get-tuple-element.787), channel_id=1, source_target_pairs={{0,508},{4,0},{8,4},{12,8},{16,12},{20,16},{24,20},{28,24},{32,28}... | collective-permute-start | bytes 27656 | tf_op jit(solution)/shard_map/while/body/eval_jaxpr/ppermute | solution.py:36
  501.7 7.9 %collective-permute-start.2 = (bf16[4,1152]{1,0:T(4,128)(2,1)S(1)}, bf16[4,1152]{1,0:T(4,128)(2,1)S(1)}, u32[]{:S(2)}, u32[]{:S(2)}) collective-permute-start(bf16[4,1152]{1,0:T(4,128)(2,1)S(1)} %get-tuple-element.787), channel_id=1, source_target_pairs={{0,508},{4,0},{8,4},{12,8},{16,12},{20,16},{24,20},{28,24},{32,28}... | collective-permute-start | bytes 27656 | tf_op jit(solution)/shard_map/while/body/eval_jaxpr/ppermute | solution.py:36
  514.2 7.9 %collective-permute-start.2 = (bf16[4,1152]{1,0:T(4,128)(2,1)S(1)}, bf16[4,1152]{1,0:T(4,128)(2,1)S(1)}, u32[]{:S(2)}, u32[]{:S(2)}) collective-permute-start(bf16[4,1152]{1,0:T(4,128)(2,1)S(1)} %get-tuple-element.787), channel_id=1, source_target_pairs={{0,508},{4,0},{8,4},{12,8},{16,12},{20,16},{24,20},{28,24},{32,28}... | collective-permute-start | bytes 27656 | tf_op jit(solution)/shard_map/while/body/eval_jaxpr/ppermute | solution.py:36
  526.8 7.9 %collective-permute-start.2 = (bf16[4,1152]{1,0:T(4,128)(2,1)S(1)}, bf16[4,1152]{1,0:T(4,128)(2,1)S(1)}, u32[]{:S(2)}, u32[]{:S(2)}) collective-permute-start(bf16[4,1152]{1,0:T(4,128)(2,1)S(1)} %get-tuple-element.787), channel_id=1, source_target_pairs={{0,508},{4,0},{8,4},{12,8},{16,12},{20,16},{24,20},{28,24},{32,28}... | collective-permute-start | bytes 27656 | tf_op jit(solution)/shard_map/while/body/eval_jaxpr/ppermute | solution.py:36
  539.4 7.9 %collective-permute-start.2 = (bf16[4,1152]{1,0:T(4,128)(2,1)S(1)}, bf16[4,1152]{1,0:T(4,128)(2,1)S(1)}, u32[]{:S(2)}, u32[]{:S(2)}) collective-permute-start(bf16[4,1152]{1,0:T(4,128)(2,1)S(1)} %get-tuple-element.787), channel_id=1, source_target_pairs={{0,508},{4,0},{8,4},{12,8},{16,12},{20,16},{24,20},{28,24},{32,28}... | collective-permute-start | bytes 27656 | tf_op jit(solution)/shard_map/while/body/eval_jaxpr/ppermute | solution.py:36
  553.9 6.4 %collective-permute-start.4 = (f32[4,1152]{1,0:T(4,128)S(1)}, f32[4,1152]{1,0:T(4,128)S(1)}, u32[]{:S(2)}, u32[]{:S(2)}) collective-permute-start(f32[4,1152]{1,0:T(4,128)S(1)} %get-tuple-element.496), channel_id=1, source_target_pairs={{0,448},{4,452},{8,456},{12,460},{16,464},{20,468},{24,472},{28,47... | collective-permute-start | bytes 55304 | tf_op jit(solution)/shard_map/ppermute | solution.py:36
  561.1 45.8 %all-to-all-start = ((f32[4,16,288]{2,1,0:T(8,128)}), f32[4,16,288]{2,1,0:T(8,128)S(1)}, u32[]{:S(2)}, u32[]{:S(2)}) async-start(f32[4,16,288]{2,1,0:T(8,128)} %copy.32), calls=%async_computation | async-start | bytes 196608 | tf_op jit(solution)/shard_map/all_to_all | solution.py:46
  607.5 6.6 %all-to-all-done = f32[4,16,288]{2,1,0:T(8,128)S(1)} async-done(((f32[4,16,288]{2,1,0:T(8,128)}), f32[4,16,288]{2,1,0:T(8,128)S(1)}, u32[]{:S(2)}, u32[]{:S(2)}) %all-to-all-start) | async-done | bytes 73760 | tf_op jit(solution)/shard_map/all_to_all | solution.py:46
  (303 shorter events, 159.3 us)
Async XLA Ops:
  140.0 10.4 %collective-permute-start = (bf16[4,1152]{1,0:T(4,128)(2,1)S(1)}, bf16[4,1152]{1,0:T(4,128)(2,1)S(1)}, u32[]{:S(2)}, u32[]{:S(2)}) collective-permute-start(bf16[4,1152]{1,0:T(4,128)(2,1)S(1)} %copy.38), channel_id=1, source_target_pairs={{0,4},{4,8},{8,12},{12,16},{16,20},{20,24},{24,28},{28,32},{32,36}... | collective-permute-start | bytes 27656 | tf_op jit(solution)/shard_map/while/body/eval_jaxpr/ppermute | solution.py:36
  143.9 10.5 %collective-permute-start.1 = (f32[4,1152]{1,0:T(4,128)S(1)}, f32[4,1152]{1,0:T(4,128)S(1)}, u32[]{:S(2)}, u32[]{:S(2)}) collective-permute-start(f32[4,1152]{1,0:T(4,128)S(1)} %convolution_add_fusion.8), channel_id=1, source_target_pairs={{0,4},{4,8},{8,12},{12,16},{16,20},{20,24},{24,28},{28,32},{32,36}... | collective-permute-start | bytes 55304 | tf_op jit(solution)/shard_map/while/body/eval_jaxpr/ppermute | solution.py:36
  154.4 10.4 %collective-permute-start = (bf16[4,1152]{1,0:T(4,128)(2,1)S(1)}, bf16[4,1152]{1,0:T(4,128)(2,1)S(1)}, u32[]{:S(2)}, u32[]{:S(2)}) collective-permute-start(bf16[4,1152]{1,0:T(4,128)(2,1)S(1)} %copy.38), channel_id=1, source_target_pairs={{0,4},{4,8},{8,12},{12,16},{16,20},{20,24},{24,28},{28,32},{32,36}... | collective-permute-start | bytes 27656 | tf_op jit(solution)/shard_map/while/body/eval_jaxpr/ppermute | solution.py:36
  157.3 10.5 %collective-permute-start.1 = (f32[4,1152]{1,0:T(4,128)S(1)}, f32[4,1152]{1,0:T(4,128)S(1)}, u32[]{:S(2)}, u32[]{:S(2)}) collective-permute-start(f32[4,1152]{1,0:T(4,128)S(1)} %convolution_add_fusion.8), channel_id=1, source_target_pairs={{0,4},{4,8},{8,12},{12,16},{16,20},{20,24},{24,28},{28,32},{32,36}... | collective-permute-start | bytes 55304 | tf_op jit(solution)/shard_map/while/body/eval_jaxpr/ppermute | solution.py:36
  167.8 10.4 %collective-permute-start = (bf16[4,1152]{1,0:T(4,128)(2,1)S(1)}, bf16[4,1152]{1,0:T(4,128)(2,1)S(1)}, u32[]{:S(2)}, u32[]{:S(2)}) collective-permute-start(bf16[4,1152]{1,0:T(4,128)(2,1)S(1)} %copy.38), channel_id=1, source_target_pairs={{0,4},{4,8},{8,12},{12,16},{16,20},{20,24},{24,28},{28,32},{32,36}... | collective-permute-start | bytes 27656 | tf_op jit(solution)/shard_map/while/body/eval_jaxpr/ppermute | solution.py:36
  170.7 10.5 %collective-permute-start.1 = (f32[4,1152]{1,0:T(4,128)S(1)}, f32[4,1152]{1,0:T(4,128)S(1)}, u32[]{:S(2)}, u32[]{:S(2)}) collective-permute-start(f32[4,1152]{1,0:T(4,128)S(1)} %convolution_add_fusion.8), channel_id=1, source_target_pairs={{0,4},{4,8},{8,12},{12,16},{16,20},{20,24},{24,28},{28,32},{32,36}... | collective-permute-start | bytes 55304 | tf_op jit(solution)/shard_map/while/body/eval_jaxpr/ppermute | solution.py:36
  181.2 10.4 %collective-permute-start = (bf16[4,1152]{1,0:T(4,128)(2,1)S(1)}, bf16[4,1152]{1,0:T(4,128)(2,1)S(1)}, u32[]{:S(2)}, u32[]{:S(2)}) collective-permute-start(bf16[4,1152]{1,0:T(4,128)(2,1)S(1)} %copy.38), channel_id=1, source_target_pairs={{0,4},{4,8},{8,12},{12,16},{16,20},{20,24},{24,28},{28,32},{32,36}... | collective-permute-start | bytes 27656 | tf_op jit(solution)/shard_map/while/body/eval_jaxpr/ppermute | solution.py:36
  184.0 10.5 %collective-permute-start.1 = (f32[4,1152]{1,0:T(4,128)S(1)}, f32[4,1152]{1,0:T(4,128)S(1)}, u32[]{:S(2)}, u32[]{:S(2)}) collective-permute-start(f32[4,1152]{1,0:T(4,128)S(1)} %convolution_add_fusion.8), channel_id=1, source_target_pairs={{0,4},{4,8},{8,12},{12,16},{16,20},{20,24},{24,28},{28,32},{32,36}... | collective-permute-start | bytes 55304 | tf_op jit(solution)/shard_map/while/body/eval_jaxpr/ppermute | solution.py:36
  194.6 10.4 %collective-permute-start = (bf16[4,1152]{1,0:T(4,128)(2,1)S(1)}, bf16[4,1152]{1,0:T(4,128)(2,1)S(1)}, u32[]{:S(2)}, u32[]{:S(2)}) collective-permute-start(bf16[4,1152]{1,0:T(4,128)(2,1)S(1)} %copy.38), channel_id=1, source_target_pairs={{0,4},{4,8},{8,12},{12,16},{16,20},{20,24},{24,28},{28,32},{32,36}... | collective-permute-start | bytes 27656 | tf_op jit(solution)/shard_map/while/body/eval_jaxpr/ppermute | solution.py:36
  197.4 10.5 %collective-permute-start.1 = (f32[4,1152]{1,0:T(4,128)S(1)}, f32[4,1152]{1,0:T(4,128)S(1)}, u32[]{:S(2)}, u32[]{:S(2)}) collective-permute-start(f32[4,1152]{1,0:T(4,128)S(1)} %convolution_add_fusion.8), channel_id=1, source_target_pairs={{0,4},{4,8},{8,12},{12,16},{16,20},{20,24},{24,28},{28,32},{32,36}... | collective-permute-start | bytes 55304 | tf_op jit(solution)/shard_map/while/body/eval_jaxpr/ppermute | solution.py:36
  208.0 10.4 %collective-permute-start = (bf16[4,1152]{1,0:T(4,128)(2,1)S(1)}, bf16[4,1152]{1,0:T(4,128)(2,1)S(1)}, u32[]{:S(2)}, u32[]{:S(2)}) collective-permute-start(bf16[4,1152]{1,0:T(4,128)(2,1)S(1)} %copy.38), channel_id=1, source_target_pairs={{0,4},{4,8},{8,12},{12,16},{16,20},{20,24},{24,28},{28,32},{32,36}... | collective-permute-start | bytes 27656 | tf_op jit(solution)/shard_map/while/body/eval_jaxpr/ppermute | solution.py:36
  210.8 10.5 %collective-permute-start.1 = (f32[4,1152]{1,0:T(4,128)S(1)}, f32[4,1152]{1,0:T(4,128)S(1)}, u32[]{:S(2)}, u32[]{:S(2)}) collective-permute-start(f32[4,1152]{1,0:T(4,128)S(1)} %convolution_add_fusion.8), channel_id=1, source_target_pairs={{0,4},{4,8},{8,12},{12,16},{16,20},{20,24},{24,28},{28,32},{32,36}... | collective-permute-start | bytes 55304 | tf_op jit(solution)/shard_map/while/body/eval_jaxpr/ppermute | solution.py:36
  221.4 10.4 %collective-permute-start = (bf16[4,1152]{1,0:T(4,128)(2,1)S(1)}, bf16[4,1152]{1,0:T(4,128)(2,1)S(1)}, u32[]{:S(2)}, u32[]{:S(2)}) collective-permute-start(bf16[4,1152]{1,0:T(4,128)(2,1)S(1)} %copy.38), channel_id=1, source_target_pairs={{0,4},{4,8},{8,12},{12,16},{16,20},{20,24},{24,28},{28,32},{32,36}... | collective-permute-start | bytes 27656 | tf_op jit(solution)/shard_map/while/body/eval_jaxpr/ppermute | solution.py:36
  224.2 10.5 %collective-permute-start.1 = (f32[4,1152]{1,0:T(4,128)S(1)}, f32[4,1152]{1,0:T(4,128)S(1)}, u32[]{:S(2)}, u32[]{:S(2)}) collective-permute-start(f32[4,1152]{1,0:T(4,128)S(1)} %convolution_add_fusion.8), channel_id=1, source_target_pairs={{0,4},{4,8},{8,12},{12,16},{16,20},{20,24},{24,28},{28,32},{32,36}... | collective-permute-start | bytes 55304 | tf_op jit(solution)/shard_map/while/body/eval_jaxpr/ppermute | solution.py:36
  234.7 10.4 %collective-permute-start = (bf16[4,1152]{1,0:T(4,128)(2,1)S(1)}, bf16[4,1152]{1,0:T(4,128)(2,1)S(1)}, u32[]{:S(2)}, u32[]{:S(2)}) collective-permute-start(bf16[4,1152]{1,0:T(4,128)(2,1)S(1)} %copy.38), channel_id=1, source_target_pairs={{0,4},{4,8},{8,12},{12,16},{16,20},{20,24},{24,28},{28,32},{32,36}... | collective-permute-start | bytes 27656 | tf_op jit(solution)/shard_map/while/body/eval_jaxpr/ppermute | solution.py:36
  237.6 10.5 %collective-permute-start.1 = (f32[4,1152]{1,0:T(4,128)S(1)}, f32[4,1152]{1,0:T(4,128)S(1)}, u32[]{:S(2)}, u32[]{:S(2)}) collective-permute-start(f32[4,1152]{1,0:T(4,128)S(1)} %convolution_add_fusion.8), channel_id=1, source_target_pairs={{0,4},{4,8},{8,12},{12,16},{16,20},{20,24},{24,28},{28,32},{32,36}... | collective-permute-start | bytes 55304 | tf_op jit(solution)/shard_map/while/body/eval_jaxpr/ppermute | solution.py:36
  248.1 10.4 %collective-permute-start = (bf16[4,1152]{1,0:T(4,128)(2,1)S(1)}, bf16[4,1152]{1,0:T(4,128)(2,1)S(1)}, u32[]{:S(2)}, u32[]{:S(2)}) collective-permute-start(bf16[4,1152]{1,0:T(4,128)(2,1)S(1)} %copy.38), channel_id=1, source_target_pairs={{0,4},{4,8},{8,12},{12,16},{16,20},{20,24},{24,28},{28,32},{32,36}... | collective-permute-start | bytes 27656 | tf_op jit(solution)/shard_map/while/body/eval_jaxpr/ppermute | solution.py:36
  251.0 10.5 %collective-permute-start.1 = (f32[4,1152]{1,0:T(4,128)S(1)}, f32[4,1152]{1,0:T(4,128)S(1)}, u32[]{:S(2)}, u32[]{:S(2)}) collective-permute-start(f32[4,1152]{1,0:T(4,128)S(1)} %convolution_add_fusion.8), channel_id=1, source_target_pairs={{0,4},{4,8},{8,12},{12,16},{16,20},{20,24},{24,28},{28,32},{32,36}... | collective-permute-start | bytes 55304 | tf_op jit(solution)/shard_map/while/body/eval_jaxpr/ppermute | solution.py:36
  261.5 10.6 %collective-permute-start = (bf16[4,1152]{1,0:T(4,128)(2,1)S(1)}, bf16[4,1152]{1,0:T(4,128)(2,1)S(1)}, u32[]{:S(2)}, u32[]{:S(2)}) collective-permute-start(bf16[4,1152]{1,0:T(4,128)(2,1)S(1)} %copy.38), channel_id=1, source_target_pairs={{0,4},{4,8},{8,12},{12,16},{16,20},{20,24},{24,28},{28,32},{32,36}... | collective-permute-start | bytes 27656 | tf_op jit(solution)/shard_map/while/body/eval_jaxpr/ppermute | solution.py:36
  264.4 10.5 %collective-permute-start.1 = (f32[4,1152]{1,0:T(4,128)S(1)}, f32[4,1152]{1,0:T(4,128)S(1)}, u32[]{:S(2)}, u32[]{:S(2)}) collective-permute-start(f32[4,1152]{1,0:T(4,128)S(1)} %convolution_add_fusion.8), channel_id=1, source_target_pairs={{0,4},{4,8},{8,12},{12,16},{16,20},{20,24},{24,28},{28,32},{32,36}... | collective-permute-start | bytes 55304 | tf_op jit(solution)/shard_map/while/body/eval_jaxpr/ppermute | solution.py:36
  274.9 10.4 %collective-permute-start = (bf16[4,1152]{1,0:T(4,128)(2,1)S(1)}, bf16[4,1152]{1,0:T(4,128)(2,1)S(1)}, u32[]{:S(2)}, u32[]{:S(2)}) collective-permute-start(bf16[4,1152]{1,0:T(4,128)(2,1)S(1)} %copy.38), channel_id=1, source_target_pairs={{0,4},{4,8},{8,12},{12,16},{16,20},{20,24},{24,28},{28,32},{32,36}... | collective-permute-start | bytes 27656 | tf_op jit(solution)/shard_map/while/body/eval_jaxpr/ppermute | solution.py:36
  277.8 10.5 %collective-permute-start.1 = (f32[4,1152]{1,0:T(4,128)S(1)}, f32[4,1152]{1,0:T(4,128)S(1)}, u32[]{:S(2)}, u32[]{:S(2)}) collective-permute-start(f32[4,1152]{1,0:T(4,128)S(1)} %convolution_add_fusion.8), channel_id=1, source_target_pairs={{0,4},{4,8},{8,12},{12,16},{16,20},{20,24},{24,28},{28,32},{32,36}... | collective-permute-start | bytes 55304 | tf_op jit(solution)/shard_map/while/body/eval_jaxpr/ppermute | solution.py:36
  288.3 10.4 %collective-permute-start = (bf16[4,1152]{1,0:T(4,128)(2,1)S(1)}, bf16[4,1152]{1,0:T(4,128)(2,1)S(1)}, u32[]{:S(2)}, u32[]{:S(2)}) collective-permute-start(bf16[4,1152]{1,0:T(4,128)(2,1)S(1)} %copy.38), channel_id=1, source_target_pairs={{0,4},{4,8},{8,12},{12,16},{16,20},{20,24},{24,28},{28,32},{32,36}... | collective-permute-start | bytes 27656 | tf_op jit(solution)/shard_map/while/body/eval_jaxpr/ppermute | solution.py:36
  291.2 10.5 %collective-permute-start.1 = (f32[4,1152]{1,0:T(4,128)S(1)}, f32[4,1152]{1,0:T(4,128)S(1)}, u32[]{:S(2)}, u32[]{:S(2)}) collective-permute-start(f32[4,1152]{1,0:T(4,128)S(1)} %convolution_add_fusion.8), channel_id=1, source_target_pairs={{0,4},{4,8},{8,12},{12,16},{16,20},{20,24},{24,28},{28,32},{32,36}... | collective-permute-start | bytes 55304 | tf_op jit(solution)/shard_map/while/body/eval_jaxpr/ppermute | solution.py:36
  301.7 10.4 %collective-permute-start = (bf16[4,1152]{1,0:T(4,128)(2,1)S(1)}, bf16[4,1152]{1,0:T(4,128)(2,1)S(1)}, u32[]{:S(2)}, u32[]{:S(2)}) collective-permute-start(bf16[4,1152]{1,0:T(4,128)(2,1)S(1)} %copy.38), channel_id=1, source_target_pairs={{0,4},{4,8},{8,12},{12,16},{16,20},{20,24},{24,28},{28,32},{32,36}... | collective-permute-start | bytes 27656 | tf_op jit(solution)/shard_map/while/body/eval_jaxpr/ppermute | solution.py:36
  304.6 10.5 %collective-permute-start.1 = (f32[4,1152]{1,0:T(4,128)S(1)}, f32[4,1152]{1,0:T(4,128)S(1)}, u32[]{:S(2)}, u32[]{:S(2)}) collective-permute-start(f32[4,1152]{1,0:T(4,128)S(1)} %convolution_add_fusion.8), channel_id=1, source_target_pairs={{0,4},{4,8},{8,12},{12,16},{16,20},{20,24},{24,28},{28,32},{32,36}... | collective-permute-start | bytes 55304 | tf_op jit(solution)/shard_map/while/body/eval_jaxpr/ppermute | solution.py:36
  315.1 10.4 %collective-permute-start = (bf16[4,1152]{1,0:T(4,128)(2,1)S(1)}, bf16[4,1152]{1,0:T(4,128)(2,1)S(1)}, u32[]{:S(2)}, u32[]{:S(2)}) collective-permute-start(bf16[4,1152]{1,0:T(4,128)(2,1)S(1)} %copy.38), channel_id=1, source_target_pairs={{0,4},{4,8},{8,12},{12,16},{16,20},{20,24},{24,28},{28,32},{32,36}... | collective-permute-start | bytes 27656 | tf_op jit(solution)/shard_map/while/body/eval_jaxpr/ppermute | solution.py:36
  317.9 10.5 %collective-permute-start.1 = (f32[4,1152]{1,0:T(4,128)S(1)}, f32[4,1152]{1,0:T(4,128)S(1)}, u32[]{:S(2)}, u32[]{:S(2)}) collective-permute-start(f32[4,1152]{1,0:T(4,128)S(1)} %convolution_add_fusion.8), channel_id=1, source_target_pairs={{0,4},{4,8},{8,12},{12,16},{16,20},{20,24},{24,28},{28,32},{32,36}... | collective-permute-start | bytes 55304 | tf_op jit(solution)/shard_map/while/body/eval_jaxpr/ppermute | solution.py:36
  328.5 10.4 %collective-permute-start = (bf16[4,1152]{1,0:T(4,128)(2,1)S(1)}, bf16[4,1152]{1,0:T(4,128)(2,1)S(1)}, u32[]{:S(2)}, u32[]{:S(2)}) collective-permute-start(bf16[4,1152]{1,0:T(4,128)(2,1)S(1)} %copy.38), channel_id=1, source_target_pairs={{0,4},{4,8},{8,12},{12,16},{16,20},{20,24},{24,28},{28,32},{32,36}... | collective-permute-start | bytes 27656 | tf_op jit(solution)/shard_map/while/body/eval_jaxpr/ppermute | solution.py:36
  331.3 10.5 %collective-permute-start.1 = (f32[4,1152]{1,0:T(4,128)S(1)}, f32[4,1152]{1,0:T(4,128)S(1)}, u32[]{:S(2)}, u32[]{:S(2)}) collective-permute-start(f32[4,1152]{1,0:T(4,128)S(1)} %convolution_add_fusion.8), channel_id=1, source_target_pairs={{0,4},{4,8},{8,12},{12,16},{16,20},{20,24},{24,28},{28,32},{32,36}... | collective-permute-start | bytes 55304 | tf_op jit(solution)/shard_map/while/body/eval_jaxpr/ppermute | solution.py:36
  341.9 10.4 %collective-permute-start = (bf16[4,1152]{1,0:T(4,128)(2,1)S(1)}, bf16[4,1152]{1,0:T(4,128)(2,1)S(1)}, u32[]{:S(2)}, u32[]{:S(2)}) collective-permute-start(bf16[4,1152]{1,0:T(4,128)(2,1)S(1)} %copy.38), channel_id=1, source_target_pairs={{0,4},{4,8},{8,12},{12,16},{16,20},{20,24},{24,28},{28,32},{32,36}... | collective-permute-start | bytes 27656 | tf_op jit(solution)/shard_map/while/body/eval_jaxpr/ppermute | solution.py:36
  344.7 10.5 %collective-permute-start.1 = (f32[4,1152]{1,0:T(4,128)S(1)}, f32[4,1152]{1,0:T(4,128)S(1)}, u32[]{:S(2)}, u32[]{:S(2)}) collective-permute-start(f32[4,1152]{1,0:T(4,128)S(1)} %convolution_add_fusion.8), channel_id=1, source_target_pairs={{0,4},{4,8},{8,12},{12,16},{16,20},{20,24},{24,28},{28,32},{32,36}... | collective-permute-start | bytes 55304 | tf_op jit(solution)/shard_map/while/body/eval_jaxpr/ppermute | solution.py:36
  355.3 5.3 collective-permute-start.2
  358.6 4.5 collective-permute-start.3
  363.3 9.9 %collective-permute-start.2 = (bf16[4,1152]{1,0:T(4,128)(2,1)S(1)}, bf16[4,1152]{1,0:T(4,128)(2,1)S(1)}, u32[]{:S(2)}, u32[]{:S(2)}) collective-permute-start(bf16[4,1152]{1,0:T(4,128)(2,1)S(1)} %get-tuple-element.787), channel_id=1, source_target_pairs={{0,508},{4,0},{8,4},{12,8},{16,12},{20,16},{24,20},{28,24},{32,28}... | collective-permute-start | bytes 27656 | tf_op jit(solution)/shard_map/while/body/eval_jaxpr/ppermute | solution.py:36
  371.2 4.5 collective-permute-start.3
  375.8 9.9 %collective-permute-start.2 = (bf16[4,1152]{1,0:T(4,128)(2,1)S(1)}, bf16[4,1152]{1,0:T(4,128)(2,1)S(1)}, u32[]{:S(2)}, u32[]{:S(2)}) collective-permute-start(bf16[4,1152]{1,0:T(4,128)(2,1)S(1)} %get-tuple-element.787), channel_id=1, source_target_pairs={{0,508},{4,0},{8,4},{12,8},{16,12},{20,16},{24,20},{28,24},{32,28}... | collective-permute-start | bytes 27656 | tf_op jit(solution)/shard_map/while/body/eval_jaxpr/ppermute | solution.py:36
  383.8 4.5 collective-permute-start.3
  388.4 9.9 %collective-permute-start.2 = (bf16[4,1152]{1,0:T(4,128)(2,1)S(1)}, bf16[4,1152]{1,0:T(4,128)(2,1)S(1)}, u32[]{:S(2)}, u32[]{:S(2)}) collective-permute-start(bf16[4,1152]{1,0:T(4,128)(2,1)S(1)} %get-tuple-element.787), channel_id=1, source_target_pairs={{0,508},{4,0},{8,4},{12,8},{16,12},{20,16},{24,20},{28,24},{32,28}... | collective-permute-start | bytes 27656 | tf_op jit(solution)/shard_map/while/body/eval_jaxpr/ppermute | solution.py:36
  396.4 4.5 collective-permute-start.3
  401.0 9.9 %collective-permute-start.2 = (bf16[4,1152]{1,0:T(4,128)(2,1)S(1)}, bf16[4,1152]{1,0:T(4,128)(2,1)S(1)}, u32[]{:S(2)}, u32[]{:S(2)}) collective-permute-start(bf16[4,1152]{1,0:T(4,128)(2,1)S(1)} %get-tuple-element.787), channel_id=1, source_target_pairs={{0,508},{4,0},{8,4},{12,8},{16,12},{20,16},{24,20},{28,24},{32,28}... | collective-permute-start | bytes 27656 | tf_op jit(solution)/shard_map/while/body/eval_jaxpr/ppermute | solution.py:36
  409.0 4.5 collective-permute-start.3
  413.6 9.9 %collective-permute-start.2 = (bf16[4,1152]{1,0:T(4,128)(2,1)S(1)}, bf16[4,1152]{1,0:T(4,128)(2,1)S(1)}, u32[]{:S(2)}, u32[]{:S(2)}) collective-permute-start(bf16[4,1152]{1,0:T(4,128)(2,1)S(1)} %get-tuple-element.787), channel_id=1, source_target_pairs={{0,508},{4,0},{8,4},{12,8},{16,12},{20,16},{24,20},{28,24},{32,28}... | collective-permute-start | bytes 27656 | tf_op jit(solution)/shard_map/while/body/eval_jaxpr/ppermute | solution.py:36
  421.5 4.5 collective-permute-start.3
  426.2 9.9 %collective-permute-start.2 = (bf16[4,1152]{1,0:T(4,128)(2,1)S(1)}, bf16[4,1152]{1,0:T(4,128)(2,1)S(1)}, u32[]{:S(2)}, u32[]{:S(2)}) collective-permute-start(bf16[4,1152]{1,0:T(4,128)(2,1)S(1)} %get-tuple-element.787), channel_id=1, source_target_pairs={{0,508},{4,0},{8,4},{12,8},{16,12},{20,16},{24,20},{28,24},{32,28}... | collective-permute-start | bytes 27656 | tf_op jit(solution)/shard_map/while/body/eval_jaxpr/ppermute | solution.py:36
  434.1 4.5 collective-permute-start.3
  438.8 9.9 %collective-permute-start.2 = (bf16[4,1152]{1,0:T(4,128)(2,1)S(1)}, bf16[4,1152]{1,0:T(4,128)(2,1)S(1)}, u32[]{:S(2)}, u32[]{:S(2)}) collective-permute-start(bf16[4,1152]{1,0:T(4,128)(2,1)S(1)} %get-tuple-element.787), channel_id=1, source_target_pairs={{0,508},{4,0},{8,4},{12,8},{16,12},{20,16},{24,20},{28,24},{32,28}... | collective-permute-start | bytes 27656 | tf_op jit(solution)/shard_map/while/body/eval_jaxpr/ppermute | solution.py:36
  446.7 4.5 collective-permute-start.3
  451.3 9.9 %collective-permute-start.2 = (bf16[4,1152]{1,0:T(4,128)(2,1)S(1)}, bf16[4,1152]{1,0:T(4,128)(2,1)S(1)}, u32[]{:S(2)}, u32[]{:S(2)}) collective-permute-start(bf16[4,1152]{1,0:T(4,128)(2,1)S(1)} %get-tuple-element.787), channel_id=1, source_target_pairs={{0,508},{4,0},{8,4},{12,8},{16,12},{20,16},{24,20},{28,24},{32,28}... | collective-permute-start | bytes 27656 | tf_op jit(solution)/shard_map/while/body/eval_jaxpr/ppermute | solution.py:36
  459.3 4.5 collective-permute-start.3
  463.9 9.9 %collective-permute-start.2 = (bf16[4,1152]{1,0:T(4,128)(2,1)S(1)}, bf16[4,1152]{1,0:T(4,128)(2,1)S(1)}, u32[]{:S(2)}, u32[]{:S(2)}) collective-permute-start(bf16[4,1152]{1,0:T(4,128)(2,1)S(1)} %get-tuple-element.787), channel_id=1, source_target_pairs={{0,508},{4,0},{8,4},{12,8},{16,12},{20,16},{24,20},{28,24},{32,28}... | collective-permute-start | bytes 27656 | tf_op jit(solution)/shard_map/while/body/eval_jaxpr/ppermute | solution.py:36
  471.9 4.5 collective-permute-start.3
  476.5 9.9 %collective-permute-start.2 = (bf16[4,1152]{1,0:T(4,128)(2,1)S(1)}, bf16[4,1152]{1,0:T(4,128)(2,1)S(1)}, u32[]{:S(2)}, u32[]{:S(2)}) collective-permute-start(bf16[4,1152]{1,0:T(4,128)(2,1)S(1)} %get-tuple-element.787), channel_id=1, source_target_pairs={{0,508},{4,0},{8,4},{12,8},{16,12},{20,16},{24,20},{28,24},{32,28}... | collective-permute-start | bytes 27656 | tf_op jit(solution)/shard_map/while/body/eval_jaxpr/ppermute | solution.py:36
  484.5 4.5 collective-permute-start.3
  489.1 9.9 %collective-permute-start.2 = (bf16[4,1152]{1,0:T(4,128)(2,1)S(1)}, bf16[4,1152]{1,0:T(4,128)(2,1)S(1)}, u32[]{:S(2)}, u32[]{:S(2)}) collective-permute-start(bf16[4,1152]{1,0:T(4,128)(2,1)S(1)} %get-tuple-element.787), channel_id=1, source_target_pairs={{0,508},{4,0},{8,4},{12,8},{16,12},{20,16},{24,20},{28,24},{32,28}... | collective-permute-start | bytes 27656 | tf_op jit(solution)/shard_map/while/body/eval_jaxpr/ppermute | solution.py:36
  497.0 4.5 collective-permute-start.3
  501.7 9.9 %collective-permute-start.2 = (bf16[4,1152]{1,0:T(4,128)(2,1)S(1)}, bf16[4,1152]{1,0:T(4,128)(2,1)S(1)}, u32[]{:S(2)}, u32[]{:S(2)}) collective-permute-start(bf16[4,1152]{1,0:T(4,128)(2,1)S(1)} %get-tuple-element.787), channel_id=1, source_target_pairs={{0,508},{4,0},{8,4},{12,8},{16,12},{20,16},{24,20},{28,24},{32,28}... | collective-permute-start | bytes 27656 | tf_op jit(solution)/shard_map/while/body/eval_jaxpr/ppermute | solution.py:36
  514.2 9.9 %collective-permute-start.2 = (bf16[4,1152]{1,0:T(4,128)(2,1)S(1)}, bf16[4,1152]{1,0:T(4,128)(2,1)S(1)}, u32[]{:S(2)}, u32[]{:S(2)}) collective-permute-start(bf16[4,1152]{1,0:T(4,128)(2,1)S(1)} %get-tuple-element.787), channel_id=1, source_target_pairs={{0,508},{4,0},{8,4},{12,8},{16,12},{20,16},{24,20},{28,24},{32,28}... | collective-permute-start | bytes 27656 | tf_op jit(solution)/shard_map/while/body/eval_jaxpr/ppermute | solution.py:36
  526.8 9.9 %collective-permute-start.2 = (bf16[4,1152]{1,0:T(4,128)(2,1)S(1)}, bf16[4,1152]{1,0:T(4,128)(2,1)S(1)}, u32[]{:S(2)}, u32[]{:S(2)}) collective-permute-start(bf16[4,1152]{1,0:T(4,128)(2,1)S(1)} %get-tuple-element.787), channel_id=1, source_target_pairs={{0,508},{4,0},{8,4},{12,8},{16,12},{20,16},{24,20},{28,24},{32,28}... | collective-permute-start | bytes 27656 | tf_op jit(solution)/shard_map/while/body/eval_jaxpr/ppermute | solution.py:36
  539.4 9.9 %collective-permute-start.2 = (bf16[4,1152]{1,0:T(4,128)(2,1)S(1)}, bf16[4,1152]{1,0:T(4,128)(2,1)S(1)}, u32[]{:S(2)}, u32[]{:S(2)}) collective-permute-start(bf16[4,1152]{1,0:T(4,128)(2,1)S(1)} %get-tuple-element.787), channel_id=1, source_target_pairs={{0,508},{4,0},{8,4},{12,8},{16,12},{20,16},{24,20},{28,24},{32,28}... | collective-permute-start | bytes 27656 | tf_op jit(solution)/shard_map/while/body/eval_jaxpr/ppermute | solution.py:36
  547.4 4.5 collective-permute-start.3
  552.0 54.8 %collective-permute-start.5 = (f32[4,1152]{1,0:T(4,128)S(1)}, f32[4,1152]{1,0:T(4,128)S(1)}, u32[]{:S(2)}, u32[]{:S(2)}) collective-permute-start(f32[4,1152]{1,0:T(4,128)S(1)} %get-tuple-element.497), channel_id=1, source_target_pairs={{0,64},{4,68},{8,72},{12,76},{16,80},{20,84},{24,88},{28,92},{32,9... | collective-permute-start | bytes 55304 | tf_op jit(solution)/shard_map/ppermute | solution.py:36
  553.9 52.9 %collective-permute-start.4 = (f32[4,1152]{1,0:T(4,128)S(1)}, f32[4,1152]{1,0:T(4,128)S(1)}, u32[]{:S(2)}, u32[]{:S(2)}) collective-permute-start(f32[4,1152]{1,0:T(4,128)S(1)} %get-tuple-element.496), channel_id=1, source_target_pairs={{0,448},{4,452},{8,456},{12,460},{16,464},{20,468},{24,472},{28,47... | collective-permute-start | bytes 55304 | tf_op jit(solution)/shard_map/ppermute | solution.py:36
  561.1 53.0 %all-to-all-start = ((f32[4,16,288]{2,1,0:T(8,128)}), f32[4,16,288]{2,1,0:T(8,128)S(1)}, u32[]{:S(2)}, u32[]{:S(2)}) async-start(f32[4,16,288]{2,1,0:T(8,128)} %copy.32), calls=%async_computation | async-start | bytes 196608 | tf_op jit(solution)/shard_map/all_to_all | solution.py:46
  (10 other events, 390.7 us)
where the time goes:
time: 618 us; the launch traced here: 615 us
  starting transfers between devices  269 us (44%)
  waiting for transfers between devices  165 us (27%)
  blocking collectives  133 us (22%)
  matrix products  36.3 us (6%)
    ppermute x66, starting transfers between devices, from_behind(): return lax.ppermute(value, axis, pairs)  223 us
    ppermute x66, waiting for transfers between devices, from_behind(): return lax.ppermute(value, axis, pairs)  158 us
    all_gather x10, blocking collectives, stacked_from(): pieces = lax.all_gather(pieces, axes[k], axis=0, tiled=True)  133 us
    all_to_all x1, starting transfers between devices, sent_and_summed(): lax.all_to_all(pieces, axis, split_axis=0, concat_axis=0, tiled=True)  45.8 us
    dot_general x32, matrix products, block_update(): lax.dot_general(image, text, (((1,), (1,)), ((), ())), preferred_element_...  24.9 us
  transfers between devices with their start and end apart: 67, of which 49 were waited for; matrix products, arithmetic and copies ran while one was open for 6% of the time, Pallas kernels for 0%

commit v1 on v0

--- a/solution.py
+++ b/solution.py
@@ -10,6 +10,13 @@
 epsilon = 1e-06
 
 
+def fit_levels_all_by_axis(dev_axis, incoming_x):
+    in_order = []
+    for _ in range(lax.axis_size(dev_axis)):
+        in_order.append(incoming_x)
+    return jnp.concatenate(lax.all_to_all(jnp.stack(in_order, axis=0), dev_axis, 0, 0), axis=0)
+
+
 def joined_along(pieces, dim):
     lengths = list(pieces.shape[1:])
     lengths[dim] *= pieces.shape[0]
@@ -19,7 +26,7 @@
 def stacked_from(x, axes, order):
     pieces = x[None]
     for k in order:
-        pieces = lax.all_gather(pieces, axes[k], axis=0, tiled=True)
+        pieces = fit_levels_all_by_axis(axes[k], incoming_x=pieces)
     current = [lax.axis_size(axes[k]) for k in reversed(order)]
     pieces = pieces.reshape(*current, *x.shape)
     turned = sorted(range(len(order)), key=lambda place: order[len(order) - 1 - place])

time: 618 us -> 599 us (0.969)
  blocking collectives: 133 us -> 27.6 us
  waiting for transfers between devices: 165 us -> 214 us
  starting transfers between devices: 269 us -> 297 us
  local copies, waits for them, and re-layouts: 4.98 us -> 12.4 us
    all_gather x10 -> x0, blocking collectives: 133 us -> none  [stacked_from(): pieces = lax.all_gather(pieces, axes[k], axis=0, tiled=True)]
    all_to_all x0 -> x7, waiting for transfers between devices: none -> 48.7 us  [fit_levels_all_by_axis(): lax.all_to_all(jnp.stack(in_order, axis=0), dev_axis, 0, 0)]
    all_to_all x0 -> x7, starting transfers between devices: none -> 32.3 us  [fit_levels_all_by_axis(): lax.all_to_all(jnp.stack(in_order, axis=0), dev_axis, 0, 0)]
    all_to_all x0 -> x3, blocking collectives: none -> 27.6 us  [fit_levels_all_by_axis(): lax.all_to_all(jnp.stack(in_order, axis=0), dev_axis, 0, 0)]
    another operation x0 -> x10, local copies, waits for them, and re-layouts: none -> 6.31 us  [fit_levels_all_by_axis(): jnp.stack(in_order, axis=0)]
  transfers between devices with their start and end apart: 67 -> 74, of which waited for: 49 -> 56; matrix products, arithmetic and copies ran while one was open for 6% -> 7% of each run, Pallas kernels for 0% -> 0%
where the time goes in v1:
time: 599 us; the launch traced here: 595 us
  starting transfers between devices  297 us (50%)
  waiting for transfers between devices  214 us (36%)
  matrix products  37.5 us (6%)
  blocking collectives  27.6 us (5%)
  local copies, waits for them, and re-layouts  12.4 us (2%)
    ppermute x66, starting transfers between devices, from_behind(): return lax.ppermute(value, axis, pairs)  223 us
    ppermute x66, waiting for transfers between devices, from_behind(): return lax.ppermute(value, axis, pairs)  158 us
    all_to_all x7, waiting for transfers between devices, fit_levels_all_by_axis(): lax.all_to_all(jnp.stack(in_order, axis=0), dev_axis, 0, 0)  48.7 us
    all_to_all x1, starting transfers between devices, sent_and_summed(): lax.all_to_all(pieces, axis, split_axis=0, concat_axis=0, tiled=True)  42 us
    all_to_all x7, starting transfers between devices, fit_levels_all_by_axis(): lax.all_to_all(jnp.stack(in_order, axis=0), dev_axis, 0, 0)  32.3 us
    all_to_all x3, blocking collectives, fit_levels_all_by_axis(): lax.all_to_all(jnp.stack(in_order, axis=0), dev_axis, 0, 0)  27.6 us
    dot_general x32, matrix products, block_update(): lax.dot_general(image, text, (((1,), (1,)), ((), ())), preferred_element_...  24.8 us
  transfers between devices with their start and end apart: 74, of which 56 were waited for; matrix products, arithmetic and copies ran while one was open for 7% of the time, Pallas kernels for 0%

profile of v1, /device:TPU:1, one launch (start us, length us, event | category | flops | bytes accessed | tf_op | source)
XLA Modules:
  0.0 595.5 jit_solution(13718331269141001594)
XLA Ops:
  1.4 9.7 %all_to_all.55 = bf16[4,1,12,288]{3,2,1,0:T(8,128)(2,1)S(1)} all-to-all(bf16[4,1,12,288]{3,2,1,0:T(8,128)(2,1)S(1)} %stack.30), channel_id=1, replica_groups=mesh['batch_0'=4,'batch_1'=4,'batch_2'=8,'mp_0'=2,'mp_1'=2] {'batch_1'}, dimensions={0} | all-to-all | bytes 55296 | tf_op jit(solution)/shard_map/all_to_all | solution.py:17
  12.5 3.3 all-to-all-start.5
  15.8 4.5 all-to-all-done.5
  21.0 10.0 %all-to-all-start.1 = ((bf16[8,4,12,288]{3,1,2,0:T(4,128)(2,1)}), bf16[8,4,12,288]{3,1,2,0:T(4,128)(2,1)S(1)}, u32[]{:S(2)}, u32[]{:S(2)}) async-start(bf16[8,4,12,288]{3,1,2,0:T(4,128)(2,1)} %stack.31), calls=%async_computation.1 | async-start | bytes 589824 | tf_op jit(solution)/shard_map/all_to_all | solution.py:17
  31.1 9.8 %all-to-all-done.1 = bf16[8,4,12,288]{3,1,2,0:T(4,128)(2,1)S(1)} async-done(((bf16[8,4,12,288]{3,1,2,0:T(4,128)(2,1)}), bf16[8,4,12,288]{3,1,2,0:T(4,128)(2,1)S(1)}, u32[]{:S(2)}, u32[]{:S(2)}) %all-to-all-start.1) | async-done | bytes 221216 | tf_op jit(solution)/shard_map/all_to_all | solution.py:17
  41.7 3.4 all-to-all-start.6
  45.3 9.3 %all-to-all-done.6 = bf16[8,4,12,288]{3,1,2,0:T(4,128)(2,1)S(1)} async-done(((bf16[8,4,12,288]{3,1,2,0:T(4,128)(2,1)}), bf16[8,4,12,288]{3,1,2,0:T(4,128)(2,1)S(1)}, u32[]{:S(2)}, u32[]{:S(2)}) %all-to-all-start.6) | async-done | bytes 221216 | tf_op jit(solution)/shard_map/all_to_all | solution.py:17
  55.9 4.0 all-to-all-start.2
  60.1 10.2 %all-to-all-done.2 = bf16[4,32,12,288]{3,1,2,0:T(8,128)(2,1)S(1)} async-done(((bf16[4,32,12,288]{3,1,2,0:T(8,128)(2,1)}), bf16[4,32,12,288]{3,1,2,0:T(8,128)(2,1)S(1)}, u32[]{:S(2)}, u32[]{:S(2)}) %all-to-all-start.2) | async-done | bytes 884768 | tf_op jit(solution)/shard_map/all_to_all | solution.py:17
  71.5 3.5 all-to-all-start.7
  80.6 4.8 all-to-all-done.7
  85.5 4.8 all-to-all-start.3
  93.2 3.7 all-to-all-done.3
  96.9 12.9 %all_to_all.56 = bf16[2,2,16,288]{3,2,1,0:T(8,128)(2,1)S(1)} all-to-all(bf16[2,2,16,288]{3,2,1,0:T(8,128)(2,1)S(1)} %pad_maximum_fusion), channel_id=1, replica_groups=mesh['batch_0'=4,'batch_1'=4,'batch_2'=8,'mp_0'=2,'mp_1'=2] {'mp_1'}, dimensions={0} | all-to-all | bytes 73728 | tf_op jit(solution)/shard_map/all_to_all | solution.py:17
  109.9 3.2 all-to-all-start.8
  113.5 6.3 %all-to-all-done.8 = bf16[2,1,16,288]{3,2,1,0:T(8,128)(2,1)S(1)} async-done(((bf16[2,1,16,288]{3,2,1,0:T(8,128)(2,1)}), bf16[2,1,16,288]{3,2,1,0:T(8,128)(2,1)S(1)}, u32[]{:S(2)}, u32[]{:S(2)}) %all-to-all-start.8) | async-done | bytes 18464 | tf_op jit(solution)/shard_map/all_to_all | solution.py:17
  119.8 4.9 all_to_all.57
  125.1 214.7 %while.40 = (s32[]{:T(128)}, bf16[4,1152]{1,0:T(4,128)(2,1)S(1)}, f32[4,1152]{1,0:T(4,128)S(1)}, f32[16,1152]{1,0:T(8,128)S(1)}, s32[16]{0:T(128)S(1)}, /*index=...) while((s32[]{:T(128)}, bf16[4,1152]{1,0:T(4,128)(2,1)S(1)}, ...), condition=%wide.region_3.4_spmd.clone, body=%wide.region_2.3_spmd.clone.sunk | while | flops 484565 | bytes 406372 | solution.py:131
  130.6 5.0 collective-permute-done
  135.6 3.4 collective-permute-done.1
  143.9 5.4 collective-permute-done
  149.4 3.0 collective-permute-done.1
  157.3 5.4 collective-permute-done
  162.7 3.0 collective-permute-done.1
  170.7 5.4 collective-permute-done
  176.1 3.0 collective-permute-done.1
  184.1 5.4 collective-permute-done
  189.5 3.0 collective-permute-done.1
  197.5 5.4 collective-permute-done
  202.9 3.0 collective-permute-done.1
  210.9 5.4 collective-permute-done
  216.3 3.0 collective-permute-done.1
  224.3 5.4 collective-permute-done
  229.7 3.0 collective-permute-done.1
  237.7 5.4 collective-permute-done
  243.1 3.0 collective-permute-done.1
  251.1 5.6 collective-permute-done
  264.5 5.4 collective-permute-done
  269.9 3.0 collective-permute-done.1
  277.8 5.4 collective-permute-done
  291.2 5.4 collective-permute-done
  304.6 5.4 collective-permute-done
  318.0 5.4 collective-permute-done
  331.4 5.4 collective-permute-done
  339.8 196.7 %while.41 = (s32[]{:T(128)}, bf16[4,1152]{1,0:T(4,128)(2,1)S(1)}, f32[4,1152]{1,0:T(4,128)S(1)}, f32[16,1152]{1,0:T(8,128)S(1)}, s32[16]{0:T(128)S(1)}, /*index=...) while((s32[]{:T(128)}, bf16[4,1152]{1,0:T(4,128)(2,1)S(1)}, ...), condition=%wide.region_5.6_spmd.clone, body=%wide.region_4.5_spmd.clone.sunk | while | flops 470742 | bytes 443248 | solution.py:134
  339.8 3.4 collective-permute-start.2
  347.8 7.9 %collective-permute-start.2 = (bf16[4,1152]{1,0:T(4,128)(2,1)S(1)}, bf16[4,1152]{1,0:T(4,128)(2,1)S(1)}, u32[]{:S(2)}, u32[]{:S(2)}) collective-permute-start(bf16[4,1152]{1,0:T(4,128)(2,1)S(1)} %get-tuple-element.787), channel_id=1, source_target_pairs={{0,508},{4,0},{8,4},{12,8},{16,12},{20,16},{24,20},{28,24},{32,28}... | collective-permute-start | bytes 27656 | tf_op jit(solution)/shard_map/while/body/eval_jaxpr/ppermute | solution.py:43
  360.4 7.9 %collective-permute-start.2 = (bf16[4,1152]{1,0:T(4,128)(2,1)S(1)}, bf16[4,1152]{1,0:T(4,128)(2,1)S(1)}, u32[]{:S(2)}, u32[]{:S(2)}) collective-permute-start(bf16[4,1152]{1,0:T(4,128)(2,1)S(1)} %get-tuple-element.787), channel_id=1, source_target_pairs={{0,508},{4,0},{8,4},{12,8},{16,12},{20,16},{24,20},{28,24},{32,28}... | collective-permute-start | bytes 27656 | tf_op jit(solution)/shard_map/while/body/eval_jaxpr/ppermute | solution.py:43
  373.0 7.9 %collective-permute-start.2 = (bf16[4,1152]{1,0:T(4,128)(2,1)S(1)}, bf16[4,1152]{1,0:T(4,128)(2,1)S(1)}, u32[]{:S(2)}, u32[]{:S(2)}) collective-permute-start(bf16[4,1152]{1,0:T(4,128)(2,1)S(1)} %get-tuple-element.787), channel_id=1, source_target_pairs={{0,508},{4,0},{8,4},{12,8},{16,12},{20,16},{24,20},{28,24},{32,28}... | collective-permute-start | bytes 27656 | tf_op jit(solution)/shard_map/while/body/eval_jaxpr/ppermute | solution.py:43
  385.5 7.9 %collective-permute-start.2 = (bf16[4,1152]{1,0:T(4,128)(2,1)S(1)}, bf16[4,1152]{1,0:T(4,128)(2,1)S(1)}, u32[]{:S(2)}, u32[]{:S(2)}) collective-permute-start(bf16[4,1152]{1,0:T(4,128)(2,1)S(1)} %get-tuple-element.787), channel_id=1, source_target_pairs={{0,508},{4,0},{8,4},{12,8},{16,12},{20,16},{24,20},{28,24},{32,28}... | collective-permute-start | bytes 27656 | tf_op jit(solution)/shard_map/while/body/eval_jaxpr/ppermute | solution.py:43
  398.1 7.9 %collective-permute-start.2 = (bf16[4,1152]{1,0:T(4,128)(2,1)S(1)}, bf16[4,1152]{1,0:T(4,128)(2,1)S(1)}, u32[]{:S(2)}, u32[]{:S(2)}) collective-permute-start(bf16[4,1152]{1,0:T(4,128)(2,1)S(1)} %get-tuple-element.787), channel_id=1, source_target_pairs={{0,508},{4,0},{8,4},{12,8},{16,12},{20,16},{24,20},{28,24},{32,28}... | collective-permute-start | bytes 27656 | tf_op jit(solution)/shard_map/while/body/eval_jaxpr/ppermute | solution.py:43
  410.7 7.9 %collective-permute-start.2 = (bf16[4,1152]{1,0:T(4,128)(2,1)S(1)}, bf16[4,1152]{1,0:T(4,128)(2,1)S(1)}, u32[]{:S(2)}, u32[]{:S(2)}) collective-permute-start(bf16[4,1152]{1,0:T(4,128)(2,1)S(1)} %get-tuple-element.787), channel_id=1, source_target_pairs={{0,508},{4,0},{8,4},{12,8},{16,12},{20,16},{24,20},{28,24},{32,28}... | collective-permute-start | bytes 27656 | tf_op jit(solution)/shard_map/while/body/eval_jaxpr/ppermute | solution.py:43
  423.3 7.9 %collective-permute-start.2 = (bf16[4,1152]{1,0:T(4,128)(2,1)S(1)}, bf16[4,1152]{1,0:T(4,128)(2,1)S(1)}, u32[]{:S(2)}, u32[]{:S(2)}) collective-permute-start(bf16[4,1152]{1,0:T(4,128)(2,1)S(1)} %get-tuple-element.787), channel_id=1, source_target_pairs={{0,508},{4,0},{8,4},{12,8},{16,12},{20,16},{24,20},{28,24},{32,28}... | collective-permute-start | bytes 27656 | tf_op jit(solution)/shard_map/while/body/eval_jaxpr/ppermute | solution.py:43
  435.9 7.9 %collective-permute-start.2 = (bf16[4,1152]{1,0:T(4,128)(2,1)S(1)}, bf16[4,1152]{1,0:T(4,128)(2,1)S(1)}, u32[]{:S(2)}, u32[]{:S(2)}) collective-permute-start(bf16[4,1152]{1,0:T(4,128)(2,1)S(1)} %get-tuple-element.787), channel_id=1, source_target_pairs={{0,508},{4,0},{8,4},{12,8},{16,12},{20,16},{24,20},{28,24},{32,28}... | collective-permute-start | bytes 27656 | tf_op jit(solution)/shard_map/while/body/eval_jaxpr/ppermute | solution.py:43
  448.4 7.9 %collective-permute-start.2 = (bf16[4,1152]{1,0:T(4,128)(2,1)S(1)}, bf16[4,1152]{1,0:T(4,128)(2,1)S(1)}, u32[]{:S(2)}, u32[]{:S(2)}) collective-permute-start(bf16[4,1152]{1,0:T(4,128)(2,1)S(1)} %get-tuple-element.787), channel_id=1, source_target_pairs={{0,508},{4,0},{8,4},{12,8},{16,12},{20,16},{24,20},{28,24},{32,28}... | collective-permute-start | bytes 27656 | tf_op jit(solution)/shard_map/while/body/eval_jaxpr/ppermute | solution.py:43
  461.0 7.9 %collective-permute-start.2 = (bf16[4,1152]{1,0:T(4,128)(2,1)S(1)}, bf16[4,1152]{1,0:T(4,128)(2,1)S(1)}, u32[]{:S(2)}, u32[]{:S(2)}) collective-permute-start(bf16[4,1152]{1,0:T(4,128)(2,1)S(1)} %get-tuple-element.787), channel_id=1, source_target_pairs={{0,508},{4,0},{8,4},{12,8},{16,12},{20,16},{24,20},{28,24},{32,28}... | collective-permute-start | bytes 27656 | tf_op jit(solution)/shard_map/while/body/eval_jaxpr/ppermute | solution.py:43
  473.6 7.9 %collective-permute-start.2 = (bf16[4,1152]{1,0:T(4,128)(2,1)S(1)}, bf16[4,1152]{1,0:T(4,128)(2,1)S(1)}, u32[]{:S(2)}, u32[]{:S(2)}) collective-permute-start(bf16[4,1152]{1,0:T(4,128)(2,1)S(1)} %get-tuple-element.787), channel_id=1, source_target_pairs={{0,508},{4,0},{8,4},{12,8},{16,12},{20,16},{24,20},{28,24},{32,28}... | collective-permute-start | bytes 27656 | tf_op jit(solution)/shard_map/while/body/eval_jaxpr/ppermute | solution.py:43
  486.2 7.9 %collective-permute-start.2 = (bf16[4,1152]{1,0:T(4,128)(2,1)S(1)}, bf16[4,1152]{1,0:T(4,128)(2,1)S(1)}, u32[]{:S(2)}, u32[]{:S(2)}) collective-permute-start(bf16[4,1152]{1,0:T(4,128)(2,1)S(1)} %get-tuple-element.787), channel_id=1, source_target_pairs={{0,508},{4,0},{8,4},{12,8},{16,12},{20,16},{24,20},{28,24},{32,28}... | collective-permute-start | bytes 27656 | tf_op jit(solution)/shard_map/while/body/eval_jaxpr/ppermute | solution.py:43
  498.8 7.9 %collective-permute-start.2 = (bf16[4,1152]{1,0:T(4,128)(2,1)S(1)}, bf16[4,1152]{1,0:T(4,128)(2,1)S(1)}, u32[]{:S(2)}, u32[]{:S(2)}) collective-permute-start(bf16[4,1152]{1,0:T(4,128)(2,1)S(1)} %get-tuple-element.787), channel_id=1, source_target_pairs={{0,508},{4,0},{8,4},{12,8},{16,12},{20,16},{24,20},{28,24},{32,28}... | collective-permute-start | bytes 27656 | tf_op jit(solution)/shard_map/while/body/eval_jaxpr/ppermute | solution.py:43
  511.3 7.9 %collective-permute-start.2 = (bf16[4,1152]{1,0:T(4,128)(2,1)S(1)}, bf16[4,1152]{1,0:T(4,128)(2,1)S(1)}, u32[]{:S(2)}, u32[]{:S(2)}) collective-permute-start(bf16[4,1152]{1,0:T(4,128)(2,1)S(1)} %get-tuple-element.787), channel_id=1, source_target_pairs={{0,508},{4,0},{8,4},{12,8},{16,12},{20,16},{24,20},{28,24},{32,28}... | collective-permute-start | bytes 27656 | tf_op jit(solution)/shard_map/while/body/eval_jaxpr/ppermute | solution.py:43
  523.9 7.9 %collective-permute-start.2 = (bf16[4,1152]{1,0:T(4,128)(2,1)S(1)}, bf16[4,1152]{1,0:T(4,128)(2,1)S(1)}, u32[]{:S(2)}, u32[]{:S(2)}) collective-permute-start(bf16[4,1152]{1,0:T(4,128)(2,1)S(1)} %get-tuple-element.787), channel_id=1, source_target_pairs={{0,508},{4,0},{8,4},{12,8},{16,12},{20,16},{24,20},{28,24},{32,28}... | collective-permute-start | bytes 27656 | tf_op jit(solution)/shard_map/while/body/eval_jaxpr/ppermute | solution.py:43
  538.4 6.4 %collective-permute-start.4 = (f32[4,1152]{1,0:T(4,128)S(1)}, f32[4,1152]{1,0:T(4,128)S(1)}, u32[]{:S(2)}, u32[]{:S(2)}) collective-permute-start(f32[4,1152]{1,0:T(4,128)S(1)} %get-tuple-element.496), channel_id=1, source_target_pairs={{0,448},{4,452},{8,456},{12,460},{16,464},{20,468},{24,472},{28,47... | collective-permute-start | bytes 55304 | tf_op jit(solution)/shard_map/ppermute | solution.py:43
  545.6 42.0 %all-to-all-start.10 = ((f32[4,16,288]{2,1,0:T(8,128)}), f32[4,16,288]{2,1,0:T(8,128)S(1)}, u32[]{:S(2)}, u32[]{:S(2)}) async-start(f32[4,16,288]{2,1,0:T(8,128)} %copy.54), calls=%async_computation.10 | async-start | bytes 196608 | tf_op jit(solution)/shard_map/all_to_all | solution.py:53
  588.2 6.6 %all-to-all-done.10 = f32[4,16,288]{2,1,0:T(8,128)S(1)} async-done(((f32[4,16,288]{2,1,0:T(8,128)}), f32[4,16,288]{2,1,0:T(8,128)S(1)}, u32[]{:S(2)}, u32[]{:S(2)}) %all-to-all-start.10) | async-done | bytes 73760 | tf_op jit(solution)/shard_map/all_to_all | solution.py:53
  (317 shorter events, 189.3 us)
Async XLA Ops:
  12.5 7.8 %all-to-all-start.5 = ((bf16[4,1,12,288]{3,2,1,0:T(8,128)(2,1)}), bf16[4,1,12,288]{3,2,1,0:T(8,128)(2,1)S(1)}, u32[]{:S(2)}, u32[]{:S(2)}) async-start(bf16[4,1,12,288]{3,2,1,0:T(8,128)(2,1)} %stack.35), calls=%async_computation.5 | async-start | bytes 98304 | tf_op jit(solution)/shard_map/all_to_all | solution.py:17
  21.0 19.8 %all-to-all-start.1 = ((bf16[8,4,12,288]{3,1,2,0:T(4,128)(2,1)}), bf16[8,4,12,288]{3,1,2,0:T(4,128)(2,1)S(1)}, u32[]{:S(2)}, u32[]{:S(2)}) async-start(bf16[8,4,12,288]{3,1,2,0:T(4,128)(2,1)} %stack.31), calls=%async_computation.1 | async-start | bytes 589824 | tf_op jit(solution)/shard_map/all_to_all | solution.py:17
  41.7 13.0 %all-to-all-start.6 = ((bf16[8,4,12,288]{3,1,2,0:T(4,128)(2,1)}), bf16[8,4,12,288]{3,1,2,0:T(4,128)(2,1)S(1)}, u32[]{:S(2)}, u32[]{:S(2)}) async-start(bf16[8,4,12,288]{3,1,2,0:T(4,128)(2,1)} %stack.36), calls=%async_computation.6 | async-start | bytes 589824 | tf_op jit(solution)/shard_map/all_to_all | solution.py:17
  55.9 14.5 %all-to-all-start.2 = ((bf16[4,32,12,288]{3,1,2,0:T(8,128)(2,1)}), bf16[4,32,12,288]{3,1,2,0:T(8,128)(2,1)S(1)}, u32[]{:S(2)}, u32[]{:S(2)}) async-start(bf16[4,32,12,288]{3,1,2,0:T(8,128)(2,1)} %stack.32), calls=%async_computation.2 | async-start | bytes 2359296 | tf_op jit(solution)/shard_map/all_to_all | solution.py:17
  71.5 13.9 %all-to-all-start.7 = ((bf16[4,32,12,288]{3,1,2,0:T(8,128)(2,1)}), bf16[4,32,12,288]{3,1,2,0:T(8,128)(2,1)S(1)}, u32[]{:S(2)}, u32[]{:S(2)}) async-start(bf16[4,32,12,288]{3,1,2,0:T(8,128)(2,1)} %stack.37), calls=%async_computation.7 | async-start | bytes 2359296 | tf_op jit(solution)/shard_map/all_to_all | solution.py:17
  85.5 11.4 %all-to-all-start.3 = ((bf16[2,1,16,288]{3,2,1,0:T(8,128)(2,1)}), bf16[2,1,16,288]{3,2,1,0:T(8,128)(2,1)S(1)}, u32[]{:S(2)}, u32[]{:S(2)}) async-start(bf16[2,1,16,288]{3,2,1,0:T(8,128)(2,1)} %pad_maximum_fusion.2), calls=%async_computation.3 | async-start | bytes 49152 | tf_op jit(solution)/shard_map/all_to_all | solution.py:17
  109.9 9.9 %all-to-all-start.8 = ((bf16[2,1,16,288]{3,2,1,0:T(8,128)(2,1)}), bf16[2,1,16,288]{3,2,1,0:T(8,128)(2,1)S(1)}, u32[]{:S(2)}, u32[]{:S(2)}) async-start(bf16[2,1,16,288]{3,2,1,0:T(8,128)(2,1)} %pad_maximum_fusion.3), calls=%async_computation.8 | async-start | bytes 49152 | tf_op jit(solution)/shard_map/all_to_all | solution.py:17
  125.2 10.4 %collective-permute-start = (bf16[4,1152]{1,0:T(4,128)(2,1)S(1)}, bf16[4,1152]{1,0:T(4,128)(2,1)S(1)}, u32[]{:S(2)}, u32[]{:S(2)}) collective-permute-start(bf16[4,1152]{1,0:T(4,128)(2,1)S(1)} %copy.60), channel_id=1, source_target_pairs={{0,4},{4,8},{8,12},{12,16},{16,20},{20,24},{24,28},{28,32},{32,36}... | collective-permute-start | bytes 27656 | tf_op jit(solution)/shard_map/while/body/eval_jaxpr/ppermute | solution.py:43
  128.4 10.5 %collective-permute-start.1 = (f32[4,1152]{1,0:T(4,128)S(1)}, f32[4,1152]{1,0:T(4,128)S(1)}, u32[]{:S(2)}, u32[]{:S(2)}) collective-permute-start(f32[4,1152]{1,0:T(4,128)S(1)} %convolution_add_fusion.8), channel_id=1, source_target_pairs={{0,4},{4,8},{8,12},{12,16},{16,20},{20,24},{24,28},{28,32},{32,36}... | collective-permute-start | bytes 55304 | tf_op jit(solution)/shard_map/while/body/eval_jaxpr/ppermute | solution.py:43
  138.9 10.4 %collective-permute-start = (bf16[4,1152]{1,0:T(4,128)(2,1)S(1)}, bf16[4,1152]{1,0:T(4,128)(2,1)S(1)}, u32[]{:S(2)}, u32[]{:S(2)}) collective-permute-start(bf16[4,1152]{1,0:T(4,128)(2,1)S(1)} %copy.60), channel_id=1, source_target_pairs={{0,4},{4,8},{8,12},{12,16},{16,20},{20,24},{24,28},{28,32},{32,36}... | collective-permute-start | bytes 27656 | tf_op jit(solution)/shard_map/while/body/eval_jaxpr/ppermute | solution.py:43
  141.8 10.5 %collective-permute-start.1 = (f32[4,1152]{1,0:T(4,128)S(1)}, f32[4,1152]{1,0:T(4,128)S(1)}, u32[]{:S(2)}, u32[]{:S(2)}) collective-permute-start(f32[4,1152]{1,0:T(4,128)S(1)} %convolution_add_fusion.8), channel_id=1, source_target_pairs={{0,4},{4,8},{8,12},{12,16},{16,20},{20,24},{24,28},{28,32},{32,36}... | collective-permute-start | bytes 55304 | tf_op jit(solution)/shard_map/while/body/eval_jaxpr/ppermute | solution.py:43
  152.3 10.4 %collective-permute-start = (bf16[4,1152]{1,0:T(4,128)(2,1)S(1)}, bf16[4,1152]{1,0:T(4,128)(2,1)S(1)}, u32[]{:S(2)}, u32[]{:S(2)}) collective-permute-start(bf16[4,1152]{1,0:T(4,128)(2,1)S(1)} %copy.60), channel_id=1, source_target_pairs={{0,4},{4,8},{8,12},{12,16},{16,20},{20,24},{24,28},{28,32},{32,36}... | collective-permute-start | bytes 27656 | tf_op jit(solution)/shard_map/while/body/eval_jaxpr/ppermute | solution.py:43
  155.2 10.5 %collective-permute-start.1 = (f32[4,1152]{1,0:T(4,128)S(1)}, f32[4,1152]{1,0:T(4,128)S(1)}, u32[]{:S(2)}, u32[]{:S(2)}) collective-permute-start(f32[4,1152]{1,0:T(4,128)S(1)} %convolution_add_fusion.8), channel_id=1, source_target_pairs={{0,4},{4,8},{8,12},{12,16},{16,20},{20,24},{24,28},{28,32},{32,36}... | collective-permute-start | bytes 55304 | tf_op jit(solution)/shard_map/while/body/eval_jaxpr/ppermute | solution.py:43
  165.7 10.4 %collective-permute-start = (bf16[4,1152]{1,0:T(4,128)(2,1)S(1)}, bf16[4,1152]{1,0:T(4,128)(2,1)S(1)}, u32[]{:S(2)}, u32[]{:S(2)}) collective-permute-start(bf16[4,1152]{1,0:T(4,128)(2,1)S(1)} %copy.60), channel_id=1, source_target_pairs={{0,4},{4,8},{8,12},{12,16},{16,20},{20,24},{24,28},{28,32},{32,36}... | collective-permute-start | bytes 27656 | tf_op jit(solution)/shard_map/while/body/eval_jaxpr/ppermute | solution.py:43
  168.6 10.5 %collective-permute-start.1 = (f32[4,1152]{1,0:T(4,128)S(1)}, f32[4,1152]{1,0:T(4,128)S(1)}, u32[]{:S(2)}, u32[]{:S(2)}) collective-permute-start(f32[4,1152]{1,0:T(4,128)S(1)} %convolution_add_fusion.8), channel_id=1, source_target_pairs={{0,4},{4,8},{8,12},{12,16},{16,20},{20,24},{24,28},{28,32},{32,36}... | collective-permute-start | bytes 55304 | tf_op jit(solution)/shard_map/while/body/eval_jaxpr/ppermute | solution.py:43
  179.1 10.4 %collective-permute-start = (bf16[4,1152]{1,0:T(4,128)(2,1)S(1)}, bf16[4,1152]{1,0:T(4,128)(2,1)S(1)}, u32[]{:S(2)}, u32[]{:S(2)}) collective-permute-start(bf16[4,1152]{1,0:T(4,128)(2,1)S(1)} %copy.60), channel_id=1, source_target_pairs={{0,4},{4,8},{8,12},{12,16},{16,20},{20,24},{24,28},{28,32},{32,36}... | collective-permute-start | bytes 27656 | tf_op jit(solution)/shard_map/while/body/eval_jaxpr/ppermute | solution.py:43
  182.0 10.5 %collective-permute-start.1 = (f32[4,1152]{1,0:T(4,128)S(1)}, f32[4,1152]{1,0:T(4,128)S(1)}, u32[]{:S(2)}, u32[]{:S(2)}) collective-permute-start(f32[4,1152]{1,0:T(4,128)S(1)} %convolution_add_fusion.8), channel_id=1, source_target_pairs={{0,4},{4,8},{8,12},{12,16},{16,20},{20,24},{24,28},{28,32},{32,36}... | collective-permute-start | bytes 55304 | tf_op jit(solution)/shard_map/while/body/eval_jaxpr/ppermute | solution.py:43
  192.5 10.4 %collective-permute-start = (bf16[4,1152]{1,0:T(4,128)(2,1)S(1)}, bf16[4,1152]{1,0:T(4,128)(2,1)S(1)}, u32[]{:S(2)}, u32[]{:S(2)}) collective-permute-start(bf16[4,1152]{1,0:T(4,128)(2,1)S(1)} %copy.60), channel_id=1, source_target_pairs={{0,4},{4,8},{8,12},{12,16},{16,20},{20,24},{24,28},{28,32},{32,36}... | collective-permute-start | bytes 27656 | tf_op jit(solution)/shard_map/while/body/eval_jaxpr/ppermute | solution.py:43
  195.4 10.5 %collective-permute-start.1 = (f32[4,1152]{1,0:T(4,128)S(1)}, f32[4,1152]{1,0:T(4,128)S(1)}, u32[]{:S(2)}, u32[]{:S(2)}) collective-permute-start(f32[4,1152]{1,0:T(4,128)S(1)} %convolution_add_fusion.8), channel_id=1, source_target_pairs={{0,4},{4,8},{8,12},{12,16},{16,20},{20,24},{24,28},{28,32},{32,36}... | collective-permute-start | bytes 55304 | tf_op jit(solution)/shard_map/while/body/eval_jaxpr/ppermute | solution.py:43
  205.9 10.4 %collective-permute-start = (bf16[4,1152]{1,0:T(4,128)(2,1)S(1)}, bf16[4,1152]{1,0:T(4,128)(2,1)S(1)}, u32[]{:S(2)}, u32[]{:S(2)}) collective-permute-start(bf16[4,1152]{1,0:T(4,128)(2,1)S(1)} %copy.60), channel_id=1, source_target_pairs={{0,4},{4,8},{8,12},{12,16},{16,20},{20,24},{24,28},{28,32},{32,36}... | collective-permute-start | bytes 27656 | tf_op jit(solution)/shard_map/while/body/eval_jaxpr/ppermute | solution.py:43
  208.8 10.5 %collective-permute-start.1 = (f32[4,1152]{1,0:T(4,128)S(1)}, f32[4,1152]{1,0:T(4,128)S(1)}, u32[]{:S(2)}, u32[]{:S(2)}) collective-permute-start(f32[4,1152]{1,0:T(4,128)S(1)} %convolution_add_fusion.8), channel_id=1, source_target_pairs={{0,4},{4,8},{8,12},{12,16},{16,20},{20,24},{24,28},{28,32},{32,36}... | collective-permute-start | bytes 55304 | tf_op jit(solution)/shard_map/while/body/eval_jaxpr/ppermute | solution.py:43
  219.3 10.4 %collective-permute-start = (bf16[4,1152]{1,0:T(4,128)(2,1)S(1)}, bf16[4,1152]{1,0:T(4,128)(2,1)S(1)}, u32[]{:S(2)}, u32[]{:S(2)}) collective-permute-start(bf16[4,1152]{1,0:T(4,128)(2,1)S(1)} %copy.60), channel_id=1, source_target_pairs={{0,4},{4,8},{8,12},{12,16},{16,20},{20,24},{24,28},{28,32},{32,36}... | collective-permute-start | bytes 27656 | tf_op jit(solution)/shard_map/while/body/eval_jaxpr/ppermute | solution.py:43
  222.1 10.5 %collective-permute-start.1 = (f32[4,1152]{1,0:T(4,128)S(1)}, f32[4,1152]{1,0:T(4,128)S(1)}, u32[]{:S(2)}, u32[]{:S(2)}) collective-permute-start(f32[4,1152]{1,0:T(4,128)S(1)} %convolution_add_fusion.8), channel_id=1, source_target_pairs={{0,4},{4,8},{8,12},{12,16},{16,20},{20,24},{24,28},{28,32},{32,36}... | collective-permute-start | bytes 55304 | tf_op jit(solution)/shard_map/while/body/eval_jaxpr/ppermute | solution.py:43
  232.7 10.4 %collective-permute-start = (bf16[4,1152]{1,0:T(4,128)(2,1)S(1)}, bf16[4,1152]{1,0:T(4,128)(2,1)S(1)}, u32[]{:S(2)}, u32[]{:S(2)}) collective-permute-start(bf16[4,1152]{1,0:T(4,128)(2,1)S(1)} %copy.60), channel_id=1, source_target_pairs={{0,4},{4,8},{8,12},{12,16},{16,20},{20,24},{24,28},{28,32},{32,36}... | collective-permute-start | bytes 27656 | tf_op jit(solution)/shard_map/while/body/eval_jaxpr/ppermute | solution.py:43
  235.5 10.5 %collective-permute-start.1 = (f32[4,1152]{1,0:T(4,128)S(1)}, f32[4,1152]{1,0:T(4,128)S(1)}, u32[]{:S(2)}, u32[]{:S(2)}) collective-permute-start(f32[4,1152]{1,0:T(4,128)S(1)} %convolution_add_fusion.8), channel_id=1, source_target_pairs={{0,4},{4,8},{8,12},{12,16},{16,20},{20,24},{24,28},{28,32},{32,36}... | collective-permute-start | bytes 55304 | tf_op jit(solution)/shard_map/while/body/eval_jaxpr/ppermute | solution.py:43
  246.1 10.6 %collective-permute-start = (bf16[4,1152]{1,0:T(4,128)(2,1)S(1)}, bf16[4,1152]{1,0:T(4,128)(2,1)S(1)}, u32[]{:S(2)}, u32[]{:S(2)}) collective-permute-start(bf16[4,1152]{1,0:T(4,128)(2,1)S(1)} %copy.60), channel_id=1, source_target_pairs={{0,4},{4,8},{8,12},{12,16},{16,20},{20,24},{24,28},{28,32},{32,36}... | collective-permute-start | bytes 27656 | tf_op jit(solution)/shard_map/while/body/eval_jaxpr/ppermute | solution.py:43
  248.9 10.5 %collective-permute-start.1 = (f32[4,1152]{1,0:T(4,128)S(1)}, f32[4,1152]{1,0:T(4,128)S(1)}, u32[]{:S(2)}, u32[]{:S(2)}) collective-permute-start(f32[4,1152]{1,0:T(4,128)S(1)} %convolution_add_fusion.8), channel_id=1, source_target_pairs={{0,4},{4,8},{8,12},{12,16},{16,20},{20,24},{24,28},{28,32},{32,36}... | collective-permute-start | bytes 55304 | tf_op jit(solution)/shard_map/while/body/eval_jaxpr/ppermute | solution.py:43
  259.4 10.4 %collective-permute-start = (bf16[4,1152]{1,0:T(4,128)(2,1)S(1)}, bf16[4,1152]{1,0:T(4,128)(2,1)S(1)}, u32[]{:S(2)}, u32[]{:S(2)}) collective-permute-start(bf16[4,1152]{1,0:T(4,128)(2,1)S(1)} %copy.60), channel_id=1, source_target_pairs={{0,4},{4,8},{8,12},{12,16},{16,20},{20,24},{24,28},{28,32},{32,36}... | collective-permute-start | bytes 27656 | tf_op jit(solution)/shard_map/while/body/eval_jaxpr/ppermute | solution.py:43
  262.3 10.5 %collective-permute-start.1 = (f32[4,1152]{1,0:T(4,128)S(1)}, f32[4,1152]{1,0:T(4,128)S(1)}, u32[]{:S(2)}, u32[]{:S(2)}) collective-permute-start(f32[4,1152]{1,0:T(4,128)S(1)} %convolution_add_fusion.8), channel_id=1, source_target_pairs={{0,4},{4,8},{8,12},{12,16},{16,20},{20,24},{24,28},{28,32},{32,36}... | collective-permute-start | bytes 55304 | tf_op jit(solution)/shard_map/while/body/eval_jaxpr/ppermute | solution.py:43
  272.8 10.4 %collective-permute-start = (bf16[4,1152]{1,0:T(4,128)(2,1)S(1)}, bf16[4,1152]{1,0:T(4,128)(2,1)S(1)}, u32[]{:S(2)}, u32[]{:S(2)}) collective-permute-start(bf16[4,1152]{1,0:T(4,128)(2,1)S(1)} %copy.60), channel_id=1, source_target_pairs={{0,4},{4,8},{8,12},{12,16},{16,20},{20,24},{24,28},{28,32},{32,36}... | collective-permute-start | bytes 27656 | tf_op jit(solution)/shard_map/while/body/eval_jaxpr/ppermute | solution.py:43
  275.7 10.5 %collective-permute-start.1 = (f32[4,1152]{1,0:T(4,128)S(1)}, f32[4,1152]{1,0:T(4,128)S(1)}, u32[]{:S(2)}, u32[]{:S(2)}) collective-permute-start(f32[4,1152]{1,0:T(4,128)S(1)} %convolution_add_fusion.8), channel_id=1, source_target_pairs={{0,4},{4,8},{8,12},{12,16},{16,20},{20,24},{24,28},{28,32},{32,36}... | collective-permute-start | bytes 55304 | tf_op jit(solution)/shard_map/while/body/eval_jaxpr/ppermute | solution.py:43
  286.2 10.4 %collective-permute-start = (bf16[4,1152]{1,0:T(4,128)(2,1)S(1)}, bf16[4,1152]{1,0:T(4,128)(2,1)S(1)}, u32[]{:S(2)}, u32[]{:S(2)}) collective-permute-start(bf16[4,1152]{1,0:T(4,128)(2,1)S(1)} %copy.60), channel_id=1, source_target_pairs={{0,4},{4,8},{8,12},{12,16},{16,20},{20,24},{24,28},{28,32},{32,36}... | collective-permute-start | bytes 27656 | tf_op jit(solution)/shard_map/while/body/eval_jaxpr/ppermute | solution.py:43
  289.1 10.5 %collective-permute-start.1 = (f32[4,1152]{1,0:T(4,128)S(1)}, f32[4,1152]{1,0:T(4,128)S(1)}, u32[]{:S(2)}, u32[]{:S(2)}) collective-permute-start(f32[4,1152]{1,0:T(4,128)S(1)} %convolution_add_fusion.8), channel_id=1, source_target_pairs={{0,4},{4,8},{8,12},{12,16},{16,20},{20,24},{24,28},{28,32},{32,36}... | collective-permute-start | bytes 55304 | tf_op jit(solution)/shard_map/while/body/eval_jaxpr/ppermute | solution.py:43
  299.6 10.4 %collective-permute-start = (bf16[4,1152]{1,0:T(4,128)(2,1)S(1)}, bf16[4,1152]{1,0:T(4,128)(2,1)S(1)}, u32[]{:S(2)}, u32[]{:S(2)}) collective-permute-start(bf16[4,1152]{1,0:T(4,128)(2,1)S(1)} %copy.60), channel_id=1, source_target_pairs={{0,4},{4,8},{8,12},{12,16},{16,20},{20,24},{24,28},{28,32},{32,36}... | collective-permute-start | bytes 27656 | tf_op jit(solution)/shard_map/while/body/eval_jaxpr/ppermute | solution.py:43
  302.5 10.5 %collective-permute-start.1 = (f32[4,1152]{1,0:T(4,128)S(1)}, f32[4,1152]{1,0:T(4,128)S(1)}, u32[]{:S(2)}, u32[]{:S(2)}) collective-permute-start(f32[4,1152]{1,0:T(4,128)S(1)} %convolution_add_fusion.8), channel_id=1, source_target_pairs={{0,4},{4,8},{8,12},{12,16},{16,20},{20,24},{24,28},{28,32},{32,36}... | collective-permute-start | bytes 55304 | tf_op jit(solution)/shard_map/while/body/eval_jaxpr/ppermute | solution.py:43
  313.0 10.4 %collective-permute-start = (bf16[4,1152]{1,0:T(4,128)(2,1)S(1)}, bf16[4,1152]{1,0:T(4,128)(2,1)S(1)}, u32[]{:S(2)}, u32[]{:S(2)}) collective-permute-start(bf16[4,1152]{1,0:T(4,128)(2,1)S(1)} %copy.60), channel_id=1, source_target_pairs={{0,4},{4,8},{8,12},{12,16},{16,20},{20,24},{24,28},{28,32},{32,36}... | collective-permute-start | bytes 27656 | tf_op jit(solution)/shard_map/while/body/eval_jaxpr/ppermute | solution.py:43
  315.9 10.5 %collective-permute-start.1 = (f32[4,1152]{1,0:T(4,128)S(1)}, f32[4,1152]{1,0:T(4,128)S(1)}, u32[]{:S(2)}, u32[]{:S(2)}) collective-permute-start(f32[4,1152]{1,0:T(4,128)S(1)} %convolution_add_fusion.8), channel_id=1, source_target_pairs={{0,4},{4,8},{8,12},{12,16},{16,20},{20,24},{24,28},{28,32},{32,36}... | collective-permute-start | bytes 55304 | tf_op jit(solution)/shard_map/while/body/eval_jaxpr/ppermute | solution.py:43
  326.4 10.4 %collective-permute-start = (bf16[4,1152]{1,0:T(4,128)(2,1)S(1)}, bf16[4,1152]{1,0:T(4,128)(2,1)S(1)}, u32[]{:S(2)}, u32[]{:S(2)}) collective-permute-start(bf16[4,1152]{1,0:T(4,128)(2,1)S(1)} %copy.60), channel_id=1, source_target_pairs={{0,4},{4,8},{8,12},{12,16},{16,20},{20,24},{24,28},{28,32},{32,36}... | collective-permute-start | bytes 27656 | tf_op jit(solution)/shard_map/while/body/eval_jaxpr/ppermute | solution.py:43
  329.3 10.5 %collective-permute-start.1 = (f32[4,1152]{1,0:T(4,128)S(1)}, f32[4,1152]{1,0:T(4,128)S(1)}, u32[]{:S(2)}, u32[]{:S(2)}) collective-permute-start(f32[4,1152]{1,0:T(4,128)S(1)} %convolution_add_fusion.8), channel_id=1, source_target_pairs={{0,4},{4,8},{8,12},{12,16},{16,20},{20,24},{24,28},{28,32},{32,36}... | collective-permute-start | bytes 55304 | tf_op jit(solution)/shard_map/while/body/eval_jaxpr/ppermute | solution.py:43
  339.8 5.3 collective-permute-start.2
  343.2 4.5 collective-permute-start.3
  347.8 9.9 %collective-permute-start.2 = (bf16[4,1152]{1,0:T(4,128)(2,1)S(1)}, bf16[4,1152]{1,0:T(4,128)(2,1)S(1)}, u32[]{:S(2)}, u32[]{:S(2)}) collective-permute-start(bf16[4,1152]{1,0:T(4,128)(2,1)S(1)} %get-tuple-element.787), channel_id=1, source_target_pairs={{0,508},{4,0},{8,4},{12,8},{16,12},{20,16},{24,20},{28,24},{32,28}... | collective-permute-start | bytes 27656 | tf_op jit(solution)/shard_map/while/body/eval_jaxpr/ppermute | solution.py:43
  355.7 4.5 collective-permute-start.3
  360.4 9.9 %collective-permute-start.2 = (bf16[4,1152]{1,0:T(4,128)(2,1)S(1)}, bf16[4,1152]{1,0:T(4,128)(2,1)S(1)}, u32[]{:S(2)}, u32[]{:S(2)}) collective-permute-start(bf16[4,1152]{1,0:T(4,128)(2,1)S(1)} %get-tuple-element.787), channel_id=1, source_target_pairs={{0,508},{4,0},{8,4},{12,8},{16,12},{20,16},{24,20},{28,24},{32,28}... | collective-permute-start | bytes 27656 | tf_op jit(solution)/shard_map/while/body/eval_jaxpr/ppermute | solution.py:43
  368.3 4.5 collective-permute-start.3
  373.0 9.9 %collective-permute-start.2 = (bf16[4,1152]{1,0:T(4,128)(2,1)S(1)}, bf16[4,1152]{1,0:T(4,128)(2,1)S(1)}, u32[]{:S(2)}, u32[]{:S(2)}) collective-permute-start(bf16[4,1152]{1,0:T(4,128)(2,1)S(1)} %get-tuple-element.787), channel_id=1, source_target_pairs={{0,508},{4,0},{8,4},{12,8},{16,12},{20,16},{24,20},{28,24},{32,28}... | collective-permute-start | bytes 27656 | tf_op jit(solution)/shard_map/while/body/eval_jaxpr/ppermute | solution.py:43
  380.9 4.5 collective-permute-start.3
  385.5 9.9 %collective-permute-start.2 = (bf16[4,1152]{1,0:T(4,128)(2,1)S(1)}, bf16[4,1152]{1,0:T(4,128)(2,1)S(1)}, u32[]{:S(2)}, u32[]{:S(2)}) collective-permute-start(bf16[4,1152]{1,0:T(4,128)(2,1)S(1)} %get-tuple-element.787), channel_id=1, source_target_pairs={{0,508},{4,0},{8,4},{12,8},{16,12},{20,16},{24,20},{28,24},{32,28}... | collective-permute-start | bytes 27656 | tf_op jit(solution)/shard_map/while/body/eval_jaxpr/ppermute | solution.py:43
  393.5 4.5 collective-permute-start.3
  398.1 9.9 %collective-permute-start.2 = (bf16[4,1152]{1,0:T(4,128)(2,1)S(1)}, bf16[4,1152]{1,0:T(4,128)(2,1)S(1)}, u32[]{:S(2)}, u32[]{:S(2)}) collective-permute-start(bf16[4,1152]{1,0:T(4,128)(2,1)S(1)} %get-tuple-element.787), channel_id=1, source_target_pairs={{0,508},{4,0},{8,4},{12,8},{16,12},{20,16},{24,20},{28,24},{32,28}... | collective-permute-start | bytes 27656 | tf_op jit(solution)/shard_map/while/body/eval_jaxpr/ppermute | solution.py:43
  406.1 4.5 collective-permute-start.3
  410.7 9.9 %collective-permute-start.2 = (bf16[4,1152]{1,0:T(4,128)(2,1)S(1)}, bf16[4,1152]{1,0:T(4,128)(2,1)S(1)}, u32[]{:S(2)}, u32[]{:S(2)}) collective-permute-start(bf16[4,1152]{1,0:T(4,128)(2,1)S(1)} %get-tuple-element.787), channel_id=1, source_target_pairs={{0,508},{4,0},{8,4},{12,8},{16,12},{20,16},{24,20},{28,24},{32,28}... | collective-permute-start | bytes 27656 | tf_op jit(solution)/shard_map/while/body/eval_jaxpr/ppermute | solution.py:43
  423.3 9.9 %collective-permute-start.2 = (bf16[4,1152]{1,0:T(4,128)(2,1)S(1)}, bf16[4,1152]{1,0:T(4,128)(2,1)S(1)}, u32[]{:S(2)}, u32[]{:S(2)}) collective-permute-start(bf16[4,1152]{1,0:T(4,128)(2,1)S(1)} %get-tuple-element.787), channel_id=1, source_target_pairs={{0,508},{4,0},{8,4},{12,8},{16,12},{20,16},{24,20},{28,24},{32,28}... | collective-permute-start | bytes 27656 | tf_op jit(solution)/shard_map/while/body/eval_jaxpr/ppermute | solution.py:43
  435.9 9.9 %collective-permute-start.2 = (bf16[4,1152]{1,0:T(4,128)(2,1)S(1)}, bf16[4,1152]{1,0:T(4,128)(2,1)S(1)}, u32[]{:S(2)}, u32[]{:S(2)}) collective-permute-start(bf16[4,1152]{1,0:T(4,128)(2,1)S(1)} %get-tuple-element.787), channel_id=1, source_target_pairs={{0,508},{4,0},{8,4},{12,8},{16,12},{20,16},{24,20},{28,24},{32,28}... | collective-permute-start | bytes 27656 | tf_op jit(solution)/shard_map/while/body/eval_jaxpr/ppermute | solution.py:43
  448.4 9.9 %collective-permute-start.2 = (bf16[4,1152]{1,0:T(4,128)(2,1)S(1)}, bf16[4,1152]{1,0:T(4,128)(2,1)S(1)}, u32[]{:S(2)}, u32[]{:S(2)}) collective-permute-start(bf16[4,1152]{1,0:T(4,128)(2,1)S(1)} %get-tuple-element.787), channel_id=1, source_target_pairs={{0,508},{4,0},{8,4},{12,8},{16,12},{20,16},{24,20},{28,24},{32,28}... | collective-permute-start | bytes 27656 | tf_op jit(solution)/shard_map/while/body/eval_jaxpr/ppermute | solution.py:43
  461.0 9.9 %collective-permute-start.2 = (bf16[4,1152]{1,0:T(4,128)(2,1)S(1)}, bf16[4,1152]{1,0:T(4,128)(2,1)S(1)}, u32[]{:S(2)}, u32[]{:S(2)}) collective-permute-start(bf16[4,1152]{1,0:T(4,128)(2,1)S(1)} %get-tuple-element.787), channel_id=1, source_target_pairs={{0,508},{4,0},{8,4},{12,8},{16,12},{20,16},{24,20},{28,24},{32,28}... | collective-permute-start | bytes 27656 | tf_op jit(solution)/shard_map/while/body/eval_jaxpr/ppermute | solution.py:43
  473.6 9.9 %collective-permute-start.2 = (bf16[4,1152]{1,0:T(4,128)(2,1)S(1)}, bf16[4,1152]{1,0:T(4,128)(2,1)S(1)}, u32[]{:S(2)}, u32[]{:S(2)}) collective-permute-start(bf16[4,1152]{1,0:T(4,128)(2,1)S(1)} %get-tuple-element.787), channel_id=1, source_target_pairs={{0,508},{4,0},{8,4},{12,8},{16,12},{20,16},{24,20},{28,24},{32,28}... | collective-permute-start | bytes 27656 | tf_op jit(solution)/shard_map/while/body/eval_jaxpr/ppermute | solution.py:43
  486.2 9.9 %collective-permute-start.2 = (bf16[4,1152]{1,0:T(4,128)(2,1)S(1)}, bf16[4,1152]{1,0:T(4,128)(2,1)S(1)}, u32[]{:S(2)}, u32[]{:S(2)}) collective-permute-start(bf16[4,1152]{1,0:T(4,128)(2,1)S(1)} %get-tuple-element.787), channel_id=1, source_target_pairs={{0,508},{4,0},{8,4},{12,8},{16,12},{20,16},{24,20},{28,24},{32,28}... | collective-permute-start | bytes 27656 | tf_op jit(solution)/shard_map/while/body/eval_jaxpr/ppermute | solution.py:43
  498.8 9.9 %collective-permute-start.2 = (bf16[4,1152]{1,0:T(4,128)(2,1)S(1)}, bf16[4,1152]{1,0:T(4,128)(2,1)S(1)}, u32[]{:S(2)}, u32[]{:S(2)}) collective-permute-start(bf16[4,1152]{1,0:T(4,128)(2,1)S(1)} %get-tuple-element.787), channel_id=1, source_target_pairs={{0,508},{4,0},{8,4},{12,8},{16,12},{20,16},{24,20},{28,24},{32,28}... | collective-permute-start | bytes 27656 | tf_op jit(solution)/shard_map/while/body/eval_jaxpr/ppermute | solution.py:43
  511.3 9.9 %collective-permute-start.2 = (bf16[4,1152]{1,0:T(4,128)(2,1)S(1)}, bf16[4,1152]{1,0:T(4,128)(2,1)S(1)}, u32[]{:S(2)}, u32[]{:S(2)}) collective-permute-start(bf16[4,1152]{1,0:T(4,128)(2,1)S(1)} %get-tuple-element.787), channel_id=1, source_target_pairs={{0,508},{4,0},{8,4},{12,8},{16,12},{20,16},{24,20},{28,24},{32,28}... | collective-permute-start | bytes 27656 | tf_op jit(solution)/shard_map/while/body/eval_jaxpr/ppermute | solution.py:43
  523.9 9.9 %collective-permute-start.2 = (bf16[4,1152]{1,0:T(4,128)(2,1)S(1)}, bf16[4,1152]{1,0:T(4,128)(2,1)S(1)}, u32[]{:S(2)}, u32[]{:S(2)}) collective-permute-start(bf16[4,1152]{1,0:T(4,128)(2,1)S(1)} %get-tuple-element.787), channel_id=1, source_target_pairs={{0,508},{4,0},{8,4},{12,8},{16,12},{20,16},{24,20},{28,24},{32,28}... | collective-permute-start | bytes 27656 | tf_op jit(solution)/shard_map/while/body/eval_jaxpr/ppermute | solution.py:43
  536.5 51.1 %collective-permute-start.5 = (f32[4,1152]{1,0:T(4,128)S(1)}, f32[4,1152]{1,0:T(4,128)S(1)}, u32[]{:S(2)}, u32[]{:S(2)}) collective-permute-start(f32[4,1152]{1,0:T(4,128)S(1)} %get-tuple-element.497), channel_id=1, source_target_pairs={{0,64},{4,68},{8,72},{12,76},{16,80},{20,84},{24,88},{28,92},{32,9... | collective-permute-start | bytes 55304 | tf_op jit(solution)/shard_map/ppermute | solution.py:43
  538.4 49.2 %collective-permute-start.4 = (f32[4,1152]{1,0:T(4,128)S(1)}, f32[4,1152]{1,0:T(4,128)S(1)}, u32[]{:S(2)}, u32[]{:S(2)}) collective-permute-start(f32[4,1152]{1,0:T(4,128)S(1)} %get-tuple-element.496), channel_id=1, source_target_pairs={{0,448},{4,452},{8,456},{12,460},{16,464},{20,468},{24,472},{28,47... | collective-permute-start | bytes 55304 | tf_op jit(solution)/shard_map/ppermute | solution.py:43
  545.6 49.3 %all-to-all-start.10 = ((f32[4,16,288]{2,1,0:T(8,128)}), f32[4,16,288]{2,1,0:T(8,128)S(1)}, u32[]{:S(2)}, u32[]{:S(2)}) async-start(f32[4,16,288]{2,1,0:T(8,128)} %copy.54), calls=%async_computation.10 | async-start | bytes 196608 | tf_op jit(solution)/shard_map/all_to_all | solution.py:53
  (13 other events, 156.5 us)
